TPU v7x, 128 devices: a whole 4x4x4 slice. The times are simulated.
128 devices in a mesh: pp: 2 (over core), ep: 64 (over z, y, x).
Axes of the slice: x: 4, y: 4, z: 4, core: 2. Of those that a mesh axis runs over, the one named last changes fastest.
Arguments:
- x_fwd: bfloat16 [2, 131072, 256], P('pp', 'ep')
- ids_fwd: int32 [2, 131072, 1], P('pp', 'ep')
- gates_fwd: bfloat16 [2, 131072, 1], P('pp', 'ep')
- x_saved: bfloat16 [2, 131072, 256], P('pp', 'ep')
- grad_out: bfloat16 [2, 131072, 256], P('pp', 'ep')
- ids_bwd: int32 [2, 131072, 1], P('pp', 'ep')
- gates_bwd: bfloat16 [2, 131072, 1], P('pp', 'ep')
- w_in: bfloat16 [2, 256, 768], P('pp')
- w_out: bfloat16 [2, 768, 256], P('pp')
- w_gate: bfloat16 [2, 128, 256, 384], P('pp', 'ep')
- w_up: bfloat16 [2, 128, 256, 384], P('pp', 'ep')
- w_down: bfloat16 [2, 128, 384, 256], P('pp', 'ep')
Outputs:
- output 1: bfloat16 [2, 131072, 256], P('pp', 'ep')
- output 2: bfloat16 [2, 131072, 256], P('pp', 'ep')
- output 3: float32 [2, 256, 768], P('pp')
- output 4: float32 [2, 768, 256], P('pp')
- output 5: float32 [2, 128, 256, 384], P('pp', 'ep')
- output 6: float32 [2, 128, 256, 384], P('pp', 'ep')
- output 7: float32 [2, 128, 384, 256], P('pp', 'ep')
All inputs are finite; a program needn't handle non-finite values.
Results may differ from a plain program's by a relative error of at most 0.00833688.
Values are sent between devices in bfloat16 or wider.
A program may use at most 1 GiB of HBM per device.

v0:
```python
import jax
import jax.numpy as jnp
from jax import lax
from jax.sharding import PartitionSpec as P

EPS = 1e-6


def rms_norm(x_in):
    x_f32 = x_in.astype(jnp.float32)
    return x_f32 * lax.rsqrt(jnp.mean(x_f32 * x_f32, axis=-1, keepdims=True) + EPS)


def rms_grad(x_in, grad_in):
    x_f32 = x_in.astype(jnp.float32)
    inv_rms = lax.rsqrt(jnp.mean(x_f32 * x_f32, axis=-1, keepdims=True) + EPS)
    return inv_rms * grad_in - x_f32 * (inv_rms * inv_rms * inv_rms) * jnp.mean(grad_in * x_f32, axis=-1, keepdims=True)


def silu_grad(pre_act):
    sig_val = jax.nn.sigmoid(pre_act)
    return sig_val * (1.0 + pre_act * (1.0 - sig_val))


def dense_forward(x_in, w_in, w_out):
    normed = rms_norm(x_in).astype(jnp.bfloat16)
    pre_act = jnp.dot(normed, w_in, preferred_element_type=jnp.float32)
    hidden = jax.nn.silu(pre_act).astype(jnp.bfloat16)
    mixed_sum = x_in.astype(jnp.float32) + jnp.dot(hidden, w_out, preferred_element_type=jnp.float32)
    return mixed_sum.astype(jnp.bfloat16), normed, pre_act, hidden


def dense_backward(x_in, grad_h, normed, pre_act, hidden, w_in, w_out):
    grad_bf = grad_h.astype(jnp.bfloat16)
    grad_hid = jnp.einsum('td,fd->tf', grad_bf, w_out, preferred_element_type=jnp.float32)
    grad_pre = (grad_hid * silu_grad(pre_act)).astype(jnp.bfloat16)
    dw_out = jnp.einsum('tf,td->fd', hidden, grad_bf, preferred_element_type=jnp.float32)
    dw_in = jnp.einsum('td,tf->df', normed, grad_pre, preferred_element_type=jnp.float32)
    grad_norm = jnp.einsum('tf,df->td', grad_pre, w_in, preferred_element_type=jnp.float32)
    grad_x = (grad_h + rms_grad(x_in, grad_norm)).astype(jnp.bfloat16)
    return grad_x, dw_in, dw_out


def route_plan(route_ids, num_exp, capacity):
    top_k = route_ids.shape[-1]
    flat_ids = route_ids.reshape(-1)
    routes = flat_ids.shape[0]
    route_order = jnp.argsort(flat_ids, stable=True)
    counts = jnp.bincount(flat_ids, length=num_exp)
    start_pos = jnp.cumsum(counts) - counts
    slot_col = jnp.arange(capacity)
    is_valid = slot_col[None, :] < counts[:, None]
    src_route = route_order[jnp.minimum(start_pos[:, None] + slot_col[None, :], routes - 1)]
    slot_rank = jnp.argsort(route_order) - start_pos[flat_ids]
    route_slot = (flat_ids * capacity + slot_rank).reshape(route_ids.shape)
    return src_route // top_k, src_route, is_valid, route_slot


def gather_rows(tok_rows, src_tok, is_valid):
    picked = jnp.take(tok_rows, src_tok, axis=0)
    return jnp.where(is_valid[..., None], picked, jnp.zeros((), picked.dtype))


def expert_forward(rows_in, w_gate, w_up, w_down):
    gate_pre = jnp.einsum('emd,edf->emf', rows_in, w_gate, preferred_element_type=jnp.float32)
    up_pre = jnp.einsum('emd,edf->emf', rows_in, w_up, preferred_element_type=jnp.float32)
    act_bf = (jax.nn.silu(gate_pre) * up_pre).astype(jnp.bfloat16)
    return jnp.einsum('emf,efd->emd', act_bf, w_down, preferred_element_type=jnp.float32).astype(jnp.bfloat16)


def expert_backward(rows_in, grad_rows, w_gate, w_up, w_down):
    gate_pre = jnp.einsum('emd,edf->emf', rows_in, w_gate, preferred_element_type=jnp.float32)
    up_pre = jnp.einsum('emd,edf->emf', rows_in, w_up, preferred_element_type=jnp.float32)
    gate_act = jax.nn.silu(gate_pre)
    act_bf = (gate_act * up_pre).astype(jnp.bfloat16)
    dw_down = jnp.einsum('emf,emd->efd', act_bf, grad_rows, preferred_element_type=jnp.float32)
    grad_act = jnp.einsum('emd,efd->emf', grad_rows, w_down, preferred_element_type=jnp.float32)
    grad_gate = (grad_act * up_pre * silu_grad(gate_pre)).astype(jnp.bfloat16)
    grad_up = (grad_act * gate_act).astype(jnp.bfloat16)
    dw_gate = jnp.einsum('emd,emf->edf', rows_in, grad_gate, preferred_element_type=jnp.float32)
    dw_up = jnp.einsum('emd,emf->edf', rows_in, grad_up, preferred_element_type=jnp.float32)
    grad_in = jnp.einsum('emf,edf->emd', grad_gate, w_gate, preferred_element_type=jnp.float32) + jnp.einsum('emf,edf->emd', grad_up, w_up, preferred_element_type=jnp.float32)
    return grad_in.astype(jnp.bfloat16), dw_gate, dw_up, dw_down


def solution(mesh):
    n_ep = mesh.shape['ep']
    n_pp = mesh.shape['pp']
    tok_spec = P('pp', 'ep', None)
    dense_spec = P('pp', None, None)
    exp_spec = P('pp', 'ep', None, None)
    next_perm = [(stage, (stage + 1) % n_pp) for stage in range(n_pp)]
    prev_perm = [(stage, (stage - 1) % n_pp) for stage in range(n_pp)]

    def body(x_fwd, ids_fwd, gates_fwd, x_saved, grad_out, ids_bwd, gates_bwd, w_in, w_out, w_gate, w_up, w_down):
        x_fwd, ids_fwd, gates_fwd = x_fwd[0], ids_fwd[0], gates_fwd[0]
        x_saved, grad_out, ids_bwd, gates_bwd = x_saved[0], grad_out[0], ids_bwd[0], gates_bwd[0]
        w_in, w_out, w_gate, w_up, w_down = w_in[0], w_out[0], w_gate[0], w_up[0], w_down[0]
        tok_dev, hid_dim = x_fwd.shape
        top_k = ids_fwd.shape[1]
        num_exp = w_gate.shape[0] * n_ep
        capacity = 2 * tok_dev * top_k // num_exp

        h_fwd = dense_forward(x_fwd, w_in, w_out)[0]
        z_fwd = rms_norm(h_fwd).astype(jnp.bfloat16)
        tok_f, route_f, valid_f, slot_f = route_plan(ids_fwd, num_exp, capacity)
        recv_f = lax.all_to_all(gather_rows(z_fwd, tok_f, valid_f), 'ep', 0, 1, tiled=True)
        out_f = expert_forward(recv_f, w_gate, w_up, w_down)
        back_f = lax.all_to_all(out_f, 'ep', 1, 0, tiled=True)
        picked = jnp.take(back_f.reshape(-1, hid_dim), slot_f, axis=0)
        y_out = (h_fwd.astype(jnp.float32) + jnp.sum(picked * gates_fwd.astype(jnp.float32)[..., None], axis=1)).astype(jnp.bfloat16)

        h_bwd, normed_b, pre_b, hidden_b = dense_forward(x_saved, w_in, w_out)
        z_bwd = rms_norm(h_bwd).astype(jnp.bfloat16)
        tok_b, route_b, valid_b, slot_b = route_plan(ids_bwd, num_exp, capacity)
        slot_gate = jnp.where(valid_b, jnp.take(gates_bwd.reshape(-1), route_b, axis=0), 0)
        grad_send = (gather_rows(grad_out, tok_b, valid_b) * slot_gate[..., None].astype(jnp.float32)).astype(jnp.bfloat16)
        x_recv = lax.all_to_all(gather_rows(z_bwd, tok_b, valid_b), 'ep', 0, 1, tiled=True)
        grad_recv = lax.all_to_all(grad_send, 'ep', 0, 1, tiled=True)
        dx_rows, dw_gate, dw_up, dw_down = expert_backward(x_recv, grad_recv, w_gate, w_up, w_down)
        dx_back = lax.all_to_all(dx_rows, 'ep', 1, 0, tiled=True)
        grad_z = jnp.sum(jnp.take(dx_back.reshape(-1, hid_dim), slot_b, axis=0), axis=1, dtype=jnp.float32)
        grad_h = grad_out.astype(jnp.float32) + rms_grad(h_bwd, grad_z)
        dx_out, dw_in, dw_out = dense_backward(x_saved, grad_h, normed_b, pre_b, hidden_b, w_in, w_out)
        dw_in = lax.psum(dw_in, 'ep')
        dw_out = lax.psum(dw_out, 'ep')
        y_next = lax.ppermute(y_out, 'pp', next_perm)
        dx_prev = lax.ppermute(dx_out, 'pp', prev_perm)
        return (y_next[None], dx_prev[None], dw_in[None], dw_out[None], dw_gate[None], dw_up[None], dw_down[None])

    return jax.shard_map(body, mesh=mesh,
                         in_specs=(tok_spec, tok_spec, tok_spec, tok_spec, tok_spec, tok_spec, tok_spec, dense_spec, dense_spec, exp_spec, exp_spec, exp_spec),
                         out_specs=(tok_spec, tok_spec, dense_spec, dense_spec, exp_spec, exp_spec, exp_spec),
                         check_vma=False)
```

profile of v0, /device:TPU:1, one launch (start us, length us, event | category | flops | bytes accessed | tf_op | source)
XLA Modules:
  0.0 555.4 jit_solution(13509155138028563136)
XLA Ops:
  7.2 1.4 compare_select_fusion.8
  8.5 14.7 %scatter_custom_fusion = s32[128]{0:T(128)S(1)} fusion(s32[2048]{0:T(1024)S(1)} %bitcast.230, s32[2048]{0:T(1024)S(1)} %broadcast.402, s32[]{:T(128)} %constant.88.clone.1), kind=kCustom, calls=%fused_computation.144 | custom fusion | flops 2048 | bytes 516 | tf_op jit(solution)/shard_map/scatter-add | solution.py:49
  24.5 5.7 %sort.62 = (s32[2048]{0:T(1024)}, s32[2048]{0:T(1024)S(1)}) sort(s32[2048]{0:T(1024)} %bitcast.221, s32[2048]{0:T(1024)S(1)} %iota.36), dimensions={0}, to_apply=%region_3.4 | sort | flops 22528 | bytes 32768 | tf_op jit(solution)/shard_map/jit(argsort)/sort | solution.py:48
  30.2 23.0 %gather_fusion = s32[4096]{0:T(1024)S(1)} fusion(s32[2048]{0:T(1024)S(1)} %get-tuple-element.13, s32[4096]{0:T(1024)S(1)} %broadcast_clamp_fusion.4), kind=kCustom, calls=%fused_computation.5 | custom fusion | bytes 49152 | tf_op jit(solution)/shard_map/gather | solution.py:53
  55.6 2.2 fusion.25
  59.3 16.6 %gather_fusion.5 = bf16[4096,256]{1,0:T(8,128)(2,1)S(1)} fusion(bf16[2048,256]{1,0:T(8,128)(2,1)S(1)} %copy.58, s32[4096]{0:T(1024)} %broadcast_clamp_fusion.3), kind=kCustom, calls=%fused_computation.clone | custom fusion | bytes 4210688 | tf_op jit(solution)/shard_map/jit(_take)/gather | solution.py:60
  75.9 4.4 select_select_fusion.2
  80.3 12.4 %all-to-all-start = ((bf16[128,32,256]{2,1,0:T(8,128)(2,1)}), bf16[128,32,256]{2,1,0:T(8,128)(2,1)}, u32[]{:S(2)}, u32[]{:S(2)}) async-start(bf16[128,32,256]{2,1,0:T(8,128)(2,1)} %select_select_fusion.2), calls=%async_computation | async-start | bytes 4194304 | tf_op jit(solution)/shard_map/all_to_all | solution.py:107
  92.7 15.4 %scatter_custom_fusion.1 = s32[128]{0:T(128)S(1)} fusion(s32[2048]{0:T(1024)S(1)} %bitcast.231, s32[2048]{0:T(1024)} %copy-done.41, s32[]{:T(128)} %constant.88.clone.1), kind=kCustom, calls=%fused_computation.142 | custom fusion | flops 2048 | bytes 1024 | tf_op jit(solution)/shard_map/scatter-add | solution.py:49
  108.7 5.0 sort.64
  113.7 23.0 %gather_fusion.2 = s32[4096]{0:T(1024)S(1)} fusion(s32[2048]{0:T(1024)S(1)} %get-tuple-element.15, s32[4096]{0:T(1024)S(1)} %broadcast_clamp_fusion.2), kind=kCustom, calls=%fused_computation.7 | custom fusion | bytes 49152 | tf_op jit(solution)/shard_map/gather | solution.py:53
  137.1 25.6 %gather_fusion.3 = bf16[4096]{0:T(1024)(128)(2,1)S(1)} fusion(bf16[2048]{0:T(1024)(128)(2,1)S(1)} %reduce.4, s32[4096]{0:T(1024)S(1)} %broadcast_clamp_fusion), kind=kCustom, calls=%fused_computation.8 | custom fusion | bytes 32768 | tf_op jit(solution)/shard_map/jit(_take)/gather | solution.py:116
  162.9 1.6 copy.64
  164.5 16.9 %gather_fusion.7 = bf16[4096,256]{1,0:T(8,128)(2,1)} fusion(bf16[2048,256]{1,0:T(8,128)(2,1)S(1)} %bitcast.204, s32[4096]{0:T(1024)S(1)} %broadcast_clamp_fusion.1), kind=kCustom, calls=%fused_computation.2.clone | custom fusion | bytes 4210688 | tf_op jit(solution)/shard_map/jit(_take)/gather | solution.py:60
  182.5 6.0 %multiply_convert_fusion.7 = bf16[128,32,256]{2,1,0:T(8,128)(2,1)} fusion(bf16[128,32,256]{2,1,0:T(8,128)(2,1)} %bitcast.211, f32[128,32]{1,0:T(8,128)S(1)} %get-tuple-element.42, pred[128,32]{1,0:T(8,128)(4,1)S(1)} %get-tuple-element.43, pred[128,32]{1,0:T(8,128)(4,1)S(1)} %iota_compare_fusion), kind=kLoop, calls=%fused_computation.23 | loop fusion | flops 5242880 | bytes 4218880 | tf_op jit(solution)/shard_map/convert_element_type | solution.py:117
  188.5 10.0 %all-to-all-start.2 = ((bf16[128,32,256]{2,1,0:T(8,128)(2,1)}), bf16[128,32,256]{2,1,0:T(8,128)(2,1)}, u32[]{:S(2)}, u32[]{:S(2)}) async-start(bf16[128,32,256]{2,1,0:T(8,128)(2,1)} %multiply_convert_fusion.7), calls=%async_computation.2 | async-start | bytes 4194304 | tf_op jit(solution)/shard_map/all_to_all | solution.py:119
  198.5 4.5 multiply_convert_fusion.4
  205.7 1.2 fusion.29
  206.9 1.5 copy.68
  208.4 16.9 %gather_fusion.8 = bf16[4096,256]{1,0:T(8,128)(2,1)} fusion(bf16[2048,256]{1,0:T(8,128)(2,1)S(1)} %copy.68, s32[4096]{0:T(1024)S(1)} %broadcast_clamp_fusion.1), kind=kCustom, calls=%fused_computation.3.clone | custom fusion | bytes 4210688 | tf_op jit(solution)/shard_map/jit(_take)/gather | solution.py:60
  225.3 4.4 select_select_fusion
  229.8 1.4 all-to-all-done.2
  231.1 8.8 %all-to-all-start.3 = ((bf16[128,32,256]{2,1,0:T(8,128)(2,1)}), bf16[128,32,256]{2,1,0:T(8,128)(2,1)}, u32[]{:S(2)}, u32[]{:S(2)}) async-start(bf16[128,32,256]{2,1,0:T(8,128)(2,1)} %select_select_fusion), calls=%async_computation.3 | async-start | bytes 4194304 | tf_op jit(solution)/shard_map/all_to_all | solution.py:118
  241.3 5.0 sort.63
  246.3 5.0 sort.65
  251.4 12.6 %gather_fusion.4 = s32[2048]{0:T(1024)S(1)} fusion(s32[128]{0:T(128)S(1)} %sub.32, s32[2048]{0:T(1024)S(1)} %broadcast_clamp_fusion.7), kind=kCustom, calls=%fused_computation.9 | custom fusion | bytes 24576 | tf_op jit(solution)/shard_map/gather | solution.py:54
  264.0 12.6 %gather_fusion.1 = s32[2048]{0:T(1024)S(1)} fusion(s32[128]{0:T(128)S(1)} %sub.30, s32[2048]{0:T(1024)S(1)} %broadcast_clamp_fusion.8), kind=kCustom, calls=%fused_computation.6 | custom fusion | bytes 24576 | tf_op jit(solution)/shard_map/gather | solution.py:54
  278.5 3.2 copy.59
  281.7 3.1 copy.67
  284.8 1.8 copy.69
  286.7 1.3 fusion.56
  288.0 1.3 fusion.50
  289.2 1.7 copy-done.14
  291.4 4.0 multiply_convert_fusion.2
  295.4 1.3 fusion.54
  298.0 1.3 add_convert_fusion
  299.3 14.2 %copy.70 = bf16[2,2048,256]{2,0,1:T(2,128)(2,1)} copy(bf16[2,2048,256]{2,1,0:T(8,128)(2,1)S(1)} %add_convert_fusion) | data formatting | bytes 4194304 | tf_op jit(solution)/shard_map/convert_element_type | solution.py:83
  313.5 10.2 %all-to-all-start.4 = ((bf16[2,2048,256]{2,0,1:T(2,128)(2,1)}), bf16[2,2048,256]{2,0,1:T(2,128)(2,1)}, u32[]{:S(2)}, u32[]{:S(2)}) async-start(bf16[2,2048,256]{2,0,1:T(2,128)(2,1)} %copy.70), calls=%async_computation.4 | async-start | bytes 4194304 | tf_op jit(solution)/shard_map/all_to_all | solution.py:121
  323.7 5.5 fusion.58
  329.2 7.6 %convolution_convert_fusion = bf16[2,2048,256]{2,1,0:T(8,128)(2,1)} fusion(f32[2,2048,384]{2,1,0:T(8,128)} %fusion.58, bf16[2,2048,256]{2,1,0:T(8,128)(2,1)} %bitcast.215, bf16[1,2,384,256]{3,2,1,0:T(8,128)(2,1)} %param.27, bf16[1,2,256,384]{3,2,1,0:T(8,128)(2,1)} %param.26), kind=kOutput, calls=%fused_computation.33 | convolution fusion | flops 1621098496 | bytes 11272192 | tf_op jit(solution)/shard_map/emf,efd->emd/dot_general | solution.py:68
  336.8 5.9 %copy.60 = bf16[2,2048,256]{2,0,1:T(2,128)(2,1)} copy(bf16[2,2048,256]{2,1,0:T(8,128)(2,1)} %convolution_convert_fusion) | data formatting | bytes 4194304 | tf_op jit(solution)/shard_map/convert_element_type | solution.py:68
  342.8 2.2 convolution_bitcast_fusion.2
  345.0 2.2 convolution_bitcast_fusion.3
  347.2 9.4 %all-to-all-done.4 = bf16[2,2048,256]{2,0,1:T(2,128)(2,1)} async-done(((bf16[2,2048,256]{2,0,1:T(2,128)(2,1)}), bf16[2,2048,256]{2,0,1:T(2,128)(2,1)}, u32[]{:S(2)}, u32[]{:S(2)}) %all-to-all-start.4) | async-done | bytes 2097184 | tf_op jit(solution)/shard_map/all_to_all | solution.py:121
  356.5 8.7 %all-to-all-start.1 = ((bf16[2,2048,256]{2,0,1:T(2,128)(2,1)}), bf16[2,2048,256]{2,0,1:T(2,128)(2,1)}, u32[]{:S(2)}, u32[]{:S(2)}) async-start(bf16[2,2048,256]{2,0,1:T(2,128)(2,1)} %copy.60), calls=%async_computation.1 | async-start | bytes 4194304 | tf_op jit(solution)/shard_map/all_to_all | solution.py:109
  365.3 2.0 copy.71
  367.4 9.0 %gather_fusion.9 = bf16[2048,256]{1,0:T(8,128)(2,1)} fusion(bf16[4096,256]{1,0:T(8,128)(2,1)S(1)} %bitcast.209, s32[2048]{0:T(1024)S(1)} %copy-done.37), kind=kCustom, calls=%fused_computation.4.clone | custom fusion | bytes 2105344 | tf_op jit(solution)/shard_map/jit(_take)/gather | solution.py:122
  376.4 1.6 copy.72
  380.6 1.9 convolution_bitcast_fusion
  382.5 4.8 multiply_convert_fusion.1
  387.3 1.7 copy-done.16
  389.0 1.9 convolution_bitcast_fusion.1
  390.8 4.8 fusion.20
  395.6 3.0 all-to-all-done.1
  398.6 2.1 copy.61
  400.7 9.1 %gather_fusion.6 = bf16[2048,256]{1,0:T(8,128)(2,1)} fusion(bf16[4096,256]{1,0:T(8,128)(2,1)S(1)} %bitcast.210, s32[2048]{0:T(1024)S(1)} %copy-done.36), kind=kCustom, calls=%fused_computation.1.clone | custom fusion | bytes 2105344 | tf_op jit(solution)/shard_map/jit(_take)/gather | solution.py:110
  409.7 2.3 copy.62
  412.1 3.1 fusion.27
  415.8 4.2 fusion.19
  420.8 7.9 %fusion.32 = f32[1,2,384,256]{3,2,1,0:T(8,128)} fusion(bf16[2,2048,256]{2,1,0:T(8,128)(2,1)S(1)} %bitcast.217, f32[2,2048,384]{2,1,0:T(8,128)} %copy-done.15, f32[2,2048,384]{2,1,0:T(8,128)} %copy-done.14), kind=kOutput, calls=%fused_computation.71 | convolution fusion | flops 814743552 | bytes 15466496 | tf_op jit(solution)/shard_map/emf,emd->efd/dot_general | solution.py:76
  428.6 2.3 copy.76
  430.9 1.3 copy.77
  432.2 112.8 %all-reduce.3.cloned.1.call-done = (f32[1,256,768]{2,1,0:T(8,128)}, f32[1,768,256]{2,1,0:T(8,128)}) async-done(((f32[1,256,768]{2,1,0:T(8,128)}, f32[1,768,256]{2,1,0:T(8,128)}), (f32[1,256,768]{2,1,0:T(8,128)}, f32[1,768,256]{2,1,0:T(8,128)})) %all-reduce.3.cloned.1.call-update) | async-done | bytes 1572880 | tf_op jit(solution)/shard_map/psum | solution.py:125
  545.0 2.1 copy.84
  (165 shorter events, 19.8 us)
Async XLA Ops:
  7.2 48.4 %copy-start = (bf16[1,256,768]{2,1,0:T(8,128)(2,1)S(1)}, bf16[1,256,768]{2,1,0:T(8,128)(2,1)}, u32[]{:S(2)}) copy-start(bf16[1,256,768]{2,1,0:T(8,128)(2,1)} %param.23) | copy-start | bytes 1179652
  8.5 15.4 %copy-start.41 = (s32[2048]{0:T(1024)}, s32[2048]{0:T(1024)S(1)}, u32[]{:S(2)}) copy-start(s32[2048]{0:T(1024)S(1)} %broadcast.402) | copy-start | bytes 24580
  30.2 24.5 %copy-start.22 = (bf16[1,2048,256]{2,1,0:T(8,128)(2,1)S(1)}, bf16[1,2048,256]{2,1,0:T(8,128)(2,1)}, u32[]{:S(2)}) copy-start(bf16[1,2048,256]{2,1,0:T(8,128)(2,1)} %param.16) | copy-start | bytes 3145732
  53.3 2.3 copy-start.43
  57.8 1.0 copy-start.17
  80.3 12.4 %copy-start.27 = (s32[1,2048,1]{1,2,0:T(1,128)S(1)}, s32[1,2048,1]{1,2,0:T(1,128)}, u32[]{:S(2)}) copy-start(s32[1,2048,1]{1,2,0:T(1,128)} %param.21) | copy-start | bytes 24580
  80.3 108.2 %all-to-all-start = ((bf16[128,32,256]{2,1,0:T(8,128)(2,1)}), bf16[128,32,256]{2,1,0:T(8,128)(2,1)}, u32[]{:S(2)}, u32[]{:S(2)}) async-start(bf16[128,32,256]{2,1,0:T(8,128)(2,1)} %select_select_fusion.2), calls=%async_computation | async-start | bytes 4194304 | tf_op jit(solution)/shard_map/all_to_all | solution.py:107
  113.7 23.3 %copy-start.39 = (bf16[1,2048,1]{1,2,0:T(2,128)(2,1)S(1)}, bf16[1,2048,1]{1,2,0:T(2,128)(2,1)}, u32[]{:S(2)}) copy-start(bf16[1,2048,1]{1,2,0:T(2,128)(2,1)} %param.22) | copy-start | bytes 12292
  162.7 1.8 copy-start.1
  164.5 38.5 %copy-start.2 = (bf16[1,2048,256]{1,2,0:T(8,128)(2,1)}, bf16[1,2048,256]{1,2,0:T(8,128)(2,1)S(1)}, u32[]{:S(2)}) copy-start(bf16[1,2048,256]{1,2,0:T(8,128)(2,1)S(1)} %copy.64) | copy-start | bytes 3145732
  182.4 16.1 %copy-start.34 = (f32[2048]{0:T(1024)}, f32[2048]{0:T(1024)S(1)}, u32[]{:S(2)}) copy-start(f32[2048]{0:T(1024)S(1)} %get-tuple-element.49) | copy-start | bytes 24580
  188.5 42.7 %all-to-all-start.2 = ((bf16[128,32,256]{2,1,0:T(8,128)(2,1)}), bf16[128,32,256]{2,1,0:T(8,128)(2,1)}, u32[]{:S(2)}, u32[]{:S(2)}) async-start(bf16[128,32,256]{2,1,0:T(8,128)(2,1)} %multiply_convert_fusion.7), calls=%async_computation.2 | async-start | bytes 4194304 | tf_op jit(solution)/shard_map/all_to_all | solution.py:119
  198.5 4.5 copy-start.44
  203.0 1.8 copy-start.46
  204.7 1.0 copy-start.4
  205.4 3.0 copy-start.24
  231.1 53.7 %all-to-all-start.3 = ((bf16[128,32,256]{2,1,0:T(8,128)(2,1)}), bf16[128,32,256]{2,1,0:T(8,128)(2,1)}, u32[]{:S(2)}, u32[]{:S(2)}) async-start(bf16[128,32,256]{2,1,0:T(8,128)(2,1)} %select_select_fusion), calls=%async_computation.3 | async-start | bytes 4194304 | tf_op jit(solution)/shard_map/all_to_all | solution.py:118
  239.9 0.7 copy-start.40
  240.6 137.8 %copy-start.13 = (bf16[1,2048,256]{1,2,0:T(8,128)(2,1)}, bf16[1,2048,256]{1,2,0:T(8,128)(2,1)S(1)}, u32[]{:S(2)}) copy-start(bf16[1,2048,256]{1,2,0:T(8,128)(2,1)S(1)} %copy.63) | copy-start | bytes 3145732
  251.4 12.6 %copy-start.33 = (s32[2048,1]{0,1:T(1,128)S(1)}, s32[2048,1]{0,1:T(1,128)}, u32[]{:S(2)}) copy-start(s32[2048,1]{0,1:T(1,128)} %get-tuple-element.54) | copy-start | bytes 24580
  264.0 13.3 %copy-start.28 = (s32[1,2048,1]{1,2,0:T(1,128)S(1)}, s32[1,2048,1]{1,2,0:T(1,128)}, u32[]{:S(2)}) copy-start(s32[1,2048,1]{1,2,0:T(1,128)} %param.17) | copy-start | bytes 24580
  276.7 101.7 %copy-start.38 = (pred[2048]{0:T(1024)(128)(4,1)}, pred[2048]{0:T(1024)(128)(4,1)S(1)}, u32[]{:S(2)}) copy-start(pred[2048]{0:T(1024)(128)(4,1)S(1)} %get-tuple-element.40) | copy-start | bytes 6148
  284.8 1.8 copy-start.18
  286.7 1.3 copy-start.21
  287.9 3.0 copy-start.14
  288.0 3.2 copy-start.19
  288.0 3.5 copy-start.42
  289.2 6.2 %copy-start.15 = (f32[2,2048,384]{2,1,0:T(8,128)}, f32[2,2048,384]{2,1,0:T(8,128)S(1)}, u32[]{:S(2)}) copy-start(f32[2,2048,384]{2,1,0:T(8,128)S(1)} %fusion.50) | copy-start | bytes 18874372
  295.4 1.8 copy-start.9
  295.4 2.6 copy-start.11
  313.5 43.0 %all-to-all-start.4 = ((bf16[2,2048,256]{2,0,1:T(2,128)(2,1)}), bf16[2,2048,256]{2,0,1:T(2,128)(2,1)}, u32[]{:S(2)}, u32[]{:S(2)}) async-start(bf16[2,2048,256]{2,0,1:T(2,128)(2,1)} %copy.70), calls=%async_computation.4 | async-start | bytes 4194304 | tf_op jit(solution)/shard_map/all_to_all | solution.py:121
  336.8 5.9 %copy-start.12 = (bf16[2,2048,384]{2,1,0:T(8,128)(2,1)S(1)}, bf16[2,2048,384]{2,1,0:T(8,128)(2,1)}, u32[]{:S(2)}) copy-start(bf16[2,2048,384]{2,1,0:T(8,128)(2,1)} %copy-done.11) | copy-start | bytes 9437188
  342.8 2.2 copy-start.10
  356.5 42.1 %all-to-all-start.1 = ((bf16[2,2048,256]{2,0,1:T(2,128)(2,1)}), bf16[2,2048,256]{2,0,1:T(2,128)(2,1)}, u32[]{:S(2)}, u32[]{:S(2)}) async-start(bf16[2,2048,256]{2,0,1:T(2,128)(2,1)} %copy.60), calls=%async_computation.1 | async-start | bytes 4194304 | tf_op jit(solution)/shard_map/all_to_all | solution.py:109
  365.3 179.7 %all-reduce.3.cloned.1.call-start = ((), (), s32[]{:S(2)}) async-start(), calls=%async_computation.5 | async-start | bytes 3145728 | tf_op jit(solution)/shard_map/psum | solution.py:125
  365.3 2.1 copy-start.37
  376.4 1.6 copy-start.5
  376.4 2.1 copy-start.25
  378.0 1.4 copy-start.7
  378.0 0.7 copy-start.29
  378.4 1.0 copy-start.31
  378.7 1.9 copy-start.47
  380.6 1.9 copy-start.45
  382.5 6.5 %copy-start.3 = (bf16[1,2048,256]{1,2,0:T(8,128)(2,1)S(1)}, bf16[1,2048,256]{1,2,0:T(8,128)(2,1)}, u32[]{:S(2)}) copy-start(bf16[1,2048,256]{1,2,0:T(8,128)(2,1)} %copy-done.2) | copy-start | bytes 3145732
  382.5 6.5 %copy-start.35 = (f32[2048]{0:T(1024)S(1)}, f32[2048]{0:T(1024)}, u32[]{:S(2)}) copy-start(f32[2048]{0:T(1024)} %copy-done.34) | copy-start | bytes 24580
  387.3 1.7 copy-start.16
  398.6 2.1 copy-start.36
  412.1 3.1 copy-start.32
  412.1 3.7 copy-start.6
  412.1 3.7 copy-start.8
  412.1 3.7 copy-start.26
  412.1 3.7 copy-start.30
  415.1 13.5 %collective-permute-start = (bf16[2048,256]{0,1:T(8,128)(2,1)}, bf16[2048,256]{0,1:T(8,128)(2,1)}, u32[]{:S(2)}, u32[]{:S(2)}) collective-permute-start(bf16[2048,256]{0,1:T(8,128)(2,1)} %fusion.27), channel_id=1, source_target_pairs={{0,64},{64,0},{1,65},{65,1},{2,66},{66,2},{3,67},{67,3},{4,68},{68... | collective-permute-start | bytes 3145736 | tf_op jit(solution)/shard_map/ppermute | solution.py:127
  415.8 5.0 copy-start.20
  420.0 10.9 %collective-permute-start.1 = (bf16[2048,256]{0,1:T(8,128)(2,1)}, bf16[2048,256]{0,1:T(8,128)(2,1)S(1)}, u32[]{:S(2)}, u32[]{:S(2)}) collective-permute-start(bf16[2048,256]{0,1:T(8,128)(2,1)} %fusion.19), channel_id=1, source_target_pairs={{0,64},{64,0},{1,65},{65,1},{2,66},{66,2},{3,67},{67,3},{4,68},{68... | collective-permute-start | bytes 3145736 | tf_op jit(solution)/shard_map/ppermute | solution.py:128
  545.0 2.1 copy-start.23
Sparse Core Ops, SparseCore 0:
  415.9 129.0 all-reduce.2
where the time goes:
time: 565 us; the launch traced here: 555 us
  local copies, waits for them, and re-layouts  222 us (39%)
  waiting for transfers between devices  126 us (22%)
  other arithmetic  84.7 us (15%)
  matrix products  55.6 us (10%)
  starting transfers between devices  50.8 us (9%)
  between operations  15.4 us (3%)
    psum x1, waiting for transfers between devices, body(): dw_in = lax.psum(dw_in, 'ep')  113 us
    gather x3, local copies, waits for them, and re-layouts, gather_rows(): picked = jnp.take(tok_rows, src_tok, axis=0)  50.4 us
    gather x5, local copies, waits for them, and re-layouts, route_plan(): route_order[jnp.minimum(start_pos[:, None] + slot_col[None, :], routes - 1)]  46.3 us
    scatter-add x2, other arithmetic, route_plan(): counts = jnp.bincount(flat_ids, length=num_exp)  30 us
    gather x2, local copies, waits for them, and re-layouts, body(): jnp.take(gates_bwd.reshape(-1), route_b, axis=0)  25.7 us
    gather x2, local copies, waits for them, and re-layouts, route_plan(): slot_rank = jnp.argsort(route_order) - start_pos[flat_ids]  25.2 us
    unnamed x103, local copies, waits for them, and re-layouts  17.9 us
    convert_element_type x1, local copies, waits for them, and re-layouts, expert_backward(): return (grad_in.astype(jnp.bfloat16), dw_gate, dw_up, dw_down)  14.2 us
  transfers between devices with their start and end apart: 8, of which 4 were waited for; matrix products, arithmetic and copies ran while one was open for 43% of the time, Pallas kernels for 0%

commit v1 on v0

v1 whole, which is shorter than its diff:
```python
import functools

import jax
import jax.numpy as jnp
from jax import lax
from jax.experimental import pallas as pl
from jax.experimental.pallas import tpu as pltpu
from jax.sharding import PartitionSpec as P

EPS = 1e-6
F32 = jnp.float32
BF16 = jnp.bfloat16
MIB = 1024 * 1024
ANY = pl.BlockSpec(memory_space=pl.ANY)
VMEM = pl.BlockSpec(memory_space=pltpu.VMEM)


def mm(a, b):
    return lax.dot_general(a, b, (((1,), (0,)), ((), ())), preferred_element_type=F32)


def mm_nt(a, b):
    return lax.dot_general(a, b, (((1,), (1,)), ((), ())), preferred_element_type=F32)


def mm_tn(a, b):
    return lax.dot_general(a, b, (((0,), (0,)), ((), ())), preferred_element_type=F32)


def inv_rms(v):
    return lax.rsqrt(jnp.mean(v * v, axis=-1, keepdims=True) + EPS)


def rms_vjp(v, inv, g):
    return inv * g - v * (inv * inv * inv) * jnp.mean(g * v, axis=-1, keepdims=True)


def plan(ids_ref, slot_ref, n_exp, cap, blk):
    tok = ids_ref.shape[1]
    upper = (lax.broadcasted_iota(jnp.int32, (blk, blk), 0) < lax.broadcasted_iota(jnp.int32, (blk, blk), 1))
    upper = jnp.where(upper, 1.0, 0.0).astype(BF16)
    expert = lax.broadcasted_iota(jnp.int32, (n_exp, blk), 0)
    carry = jnp.zeros((n_exp, 1), F32)
    for b in range(tok // blk):
        ids = ids_ref[:, b * blk:(b + 1) * blk]
        hot = jnp.where(expert == ids, 1.0, 0.0)
        before = mm(hot.astype(BF16), upper) + carry
        rank = jnp.sum(hot * before, axis=0, keepdims=True).astype(jnp.int32)
        carry = carry + jnp.sum(hot, axis=1, keepdims=True)
        slot_ref[:, b * blk:(b + 1) * blk] = (ids & 1) * (n_exp // 2 * cap) + (ids >> 1) * cap + rank


def column(row):
    n = row.shape[1]
    return jnp.transpose(jnp.broadcast_to(row, (128, n)))[:, :1]


def dispatch_chunk(slot_ref, rows_ref, start, size):
    tok = slot_ref.shape[1]
    want = lax.broadcasted_iota(jnp.int32, (size, tok), 0) + start
    pick = jnp.where(want == slot_ref[...], 1.0, 0.0).astype(BF16)
    return mm(pick, rows_ref[...]).astype(BF16)


def combine_chunk(slot_row, back_ref):
    size = slot_row.shape[1]
    slots = back_ref.shape[0]
    lane = lax.broadcasted_iota(jnp.int32, (size, slots), 1)
    pick = jnp.where(lane == column(slot_row), 1.0, 0.0).astype(BF16)
    return mm(pick, back_ref[...])


def dense_tile(x, w_in, w_out):
    inv = inv_rms(x)
    normed = (x * inv).astype(BF16)
    pre = mm(normed, w_in)
    hid = (pre * jax.nn.sigmoid(pre)).astype(BF16)
    h = (x + mm(hid, w_out)).astype(BF16)
    return h


def pre_fwd_kernel(cfg, x_ref, ids_ref, w_in_ref, w_out_ref, send_ref, h_ref, slot_ref, z_ref):
    tok, n_exp, cap, blk, chunk = cfg
    plan(ids_ref, slot_ref, n_exp, cap, blk)

    @pl.loop(0, tok // blk)
    def _(i):
        t = pl.ds(pl.multiple_of(i * blk, blk), blk)
        h = dense_tile(x_ref[t, :].astype(F32), w_in_ref[...], w_out_ref[...])
        h_ref[t, :] = h
        hf = h.astype(F32)
        z_ref[t, :] = (hf * inv_rms(hf)).astype(BF16)

    @pl.loop(0, n_exp * cap // chunk)
    def _(c):
        s = pl.multiple_of(c * chunk, chunk)
        send_ref[pl.ds(s, chunk), :] = dispatch_chunk(slot_ref, z_ref, s, chunk)


def pre_bwd_kernel(cfg, x_ref, g_ref, ids_ref, gate_ref, w_in_ref, w_out_ref, sz_ref, sd_ref, h_ref, slot_ref, zd_ref):
    tok, n_exp, cap, blk, chunk = cfg
    hid = x_ref.shape[1]
    plan(ids_ref, slot_ref, n_exp, cap, blk)

    @pl.loop(0, tok // blk)
    def _(i):
        t = pl.ds(pl.multiple_of(i * blk, blk), blk)
        h = dense_tile(x_ref[t, :].astype(F32), w_in_ref[...], w_out_ref[...])
        h_ref[t, :] = h
        hf = h.astype(F32)
        zd_ref[t, :hid] = (hf * inv_rms(hf)).astype(BF16)
        gate = column(gate_ref[:, t])
        zd_ref[t, hid:] = (gate * g_ref[t, :].astype(F32)).astype(BF16)

    @pl.loop(0, n_exp * cap // chunk)
    def _(c):
        s = pl.multiple_of(c * chunk, chunk)
        both = dispatch_chunk(slot_ref, zd_ref, s, chunk)
        sz_ref[pl.ds(s, chunk), :] = both[:, :hid]
        sd_ref[pl.ds(s, chunk), :] = both[:, hid:]


def expert_fwd_kernel(blk, x_ref, wg_ref, wu_ref, wd_ref, out_ref):
    rows = x_ref.shape[0] // 2
    for e in range(2):
        @pl.loop(0, rows // blk)
        def _(i):
            r = pl.ds(pl.multiple_of(e * rows + i * blk, blk), blk)
            x = x_ref[r, :]
            p = mm(x, wg_ref[e])
            q = mm(x, wu_ref[e])
            act = (p * jax.nn.sigmoid(p) * q).astype(BF16)
            out_ref[r, :] = mm(act, wd_ref[e]).astype(BF16)


def expert_bwd_kernel(blk, x_ref, d_ref, wg_ref, wu_ref, wd_ref, dz_ref, dwg_ref, dwu_ref, dwd_ref, acc_ref):
    rows = x_ref.shape[0] // 2
    for e in range(2):
        dwg_ref[e] = jnp.zeros(dwg_ref.shape[1:], F32)
        dwu_ref[e] = jnp.zeros(dwu_ref.shape[1:], F32)
        acc_ref[...] = jnp.zeros(acc_ref.shape, F32)

        @pl.loop(0, rows // blk)
        def _(i):
            r = pl.ds(pl.multiple_of(e * rows + i * blk, blk), blk)
            x = x_ref[r, :]
            dy = d_ref[r, :]
            p = mm(x, wg_ref[e])
            q = mm(x, wu_ref[e])
            a = mm_nt(dy, wd_ref[e])
            sig = jax.nn.sigmoid(p)
            act_g = p * sig
            act = (act_g * q).astype(BF16)
            dp = (a * q * (sig * (1.0 + p * (1.0 - sig)))).astype(BF16)
            dq = (a * act_g).astype(BF16)
            dz_ref[r, :] = (mm_nt(dp, wg_ref[e]) + mm_nt(dq, wu_ref[e])).astype(BF16)
            dwg_ref[e] += mm_tn(x, dp)
            dwu_ref[e] += mm_tn(x, dq)
            acc_ref[...] += mm_tn(dy, act)

        dwd_ref[e] = jnp.transpose(acc_ref[...])


def post_fwd_kernel(blk, back_ref, slot_ref, gate_ref, h_ref, y_ref):
    @pl.loop(0, h_ref.shape[0] // blk)
    def _(i):
        t = pl.ds(pl.multiple_of(i * blk, blk), blk)
        picked = combine_chunk(slot_ref[:, t], back_ref)
        y_ref[t, :] = (h_ref[t, :].astype(F32) + picked * column(gate_ref[:, t])).astype(BF16)


def post_bwd_kernel(blk, back_ref, slot_ref, h_ref, g_ref, x_ref, w_in_ref, w_out_ref, dx_ref, dwin_ref, dwout_ref, acc_ref):
    dwin_ref[...] = jnp.zeros(dwin_ref.shape, F32)
    acc_ref[...] = jnp.zeros(acc_ref.shape, F32)

    @pl.loop(0, h_ref.shape[0] // blk)
    def _(i):
        t = pl.ds(pl.multiple_of(i * blk, blk), blk)
        gz = combine_chunk(slot_ref[:, t], back_ref)
        h = h_ref[t, :].astype(F32)
        dh = g_ref[t, :].astype(F32) + rms_vjp(h, inv_rms(h), gz)
        b = dh.astype(BF16)
        x = x_ref[t, :].astype(F32)
        inv = inv_rms(x)
        normed = (x * inv).astype(BF16)
        pre = mm(normed, w_in_ref[...])
        sig = jax.nn.sigmoid(pre)
        hid = (pre * sig).astype(BF16)
        da = (mm_nt(b, w_out_ref[...]) * (sig * (1.0 + pre * (1.0 - sig)))).astype(BF16)
        acc_ref[...] += mm_tn(b, hid)
        dwin_ref[...] += mm_tn(normed, da)
        dx_ref[t, :] = (dh + rms_vjp(x, inv, mm_nt(da, w_in_ref[...]))).astype(BF16)

    dwout_ref[...] = jnp.transpose(acc_ref[...])


def vmem_call(kernel, outs, scratch=(), flops=0):
    return pl.pallas_call(
        kernel,
        out_shape=[jax.ShapeDtypeStruct(s, d) for s, d in outs],
        out_specs=[VMEM] * len(outs),
        scratch_shapes=list(scratch),
        compiler_params=pltpu.CompilerParams(vmem_limit_bytes=48 * MIB),
        cost_estimate=pl.CostEstimate(flops=flops, bytes_accessed=8 * MIB, transcendentals=0),
    )


def enter(n_ep):
    me = lax.axis_index('ep')
    barrier = pltpu.get_barrier_semaphore()

    @pl.loop(1, n_ep)
    def _(k):
        pl.semaphore_signal(barrier, inc=1, device_id={'ep': lax.rem(me + k, n_ep)}, device_id_type=pl.DeviceIdType.MESH)

    pl.semaphore_wait(barrier, n_ep - 1)
    return me


def peer(me, k, n_ep):
    side = round(n_ep ** (1 / 3))
    if side ** 3 != n_ep:
        return lax.rem(me + k, n_ep)
    x = lax.rem(lax.rem(me, side) + lax.rem(k, side), side)
    y = lax.rem(me // side % side + k // side % side, side)
    z = lax.rem(me // (side * side) + k // (side * side), side)
    return (z * side + y) * side + x


def exchange_kernel(n_ep, n, *refs):
    ins, outs = refs[:n], refs[n:2 * n]
    send_sem, recv_sem, local_sem = refs[2 * n:]
    me = enter(n_ep)
    for i in range(n):
        pltpu.make_async_copy(ins[i].at[:, me], outs[i].at[:, me], local_sem.at[i]).start()

    @pl.loop(1, n_ep)
    def _(k):
        to = peer(me, k, n_ep)
        for i in range(n):
            pltpu.make_async_remote_copy(
                ins[i].at[:, to], outs[i].at[:, me], send_sem.at[i], recv_sem.at[i],
                device_id={'ep': to}, device_id_type=pl.DeviceIdType.MESH).start()

    for i in range(n):
        pltpu.make_async_copy(ins[i].at[:, me], outs[i].at[:, me], local_sem.at[i]).wait()
        most = pl.ds(0, n_ep - 1)
        pltpu.make_async_copy(ins[i].at[:, most], ins[i].at[:, most], send_sem.at[i]).wait()
        pltpu.make_async_copy(outs[i].at[:, most], outs[i].at[:, most], recv_sem.at[i]).wait()


def exchange(n_ep, cid, *bufs):
    n = len(bufs)
    return pl.pallas_call(
        functools.partial(exchange_kernel, n_ep, n),
        out_shape=[jax.ShapeDtypeStruct(b.shape, b.dtype) for b in bufs],
        in_specs=[ANY] * n,
        out_specs=[ANY] * n,
        scratch_shapes=[pltpu.SemaphoreType.DMA((n,)), pltpu.SemaphoreType.DMA((n,)), pltpu.SemaphoreType.DMA((n,))],
        compiler_params=pltpu.CompilerParams(collective_id=cid, has_side_effects=True),
        cost_estimate=pl.CostEstimate(flops=10 ** 10, bytes_accessed=8 * MIB, transcendentals=0),
    )(*bufs)


def reduce_kernel(n_ep, part_ref, sum_ref):
    total = part_ref[0, 0]
    for i in range(1, n_ep):
        total = total + part_ref[0, i]
    sum_ref[...] = total


def spread_kernel(n_ep, piece_ref, out_ref, send_sem, recv_sem, local_sem):
    me = enter(n_ep)
    own = pltpu.make_async_copy(piece_ref, out_ref.at[me], local_sem)
    own.start()

    @pl.loop(1, n_ep)
    def _(k):
        to = peer(me, k, n_ep)
        pltpu.make_async_remote_copy(
            piece_ref, out_ref.at[me], send_sem, recv_sem,
            device_id={'ep': to}, device_id_type=pl.DeviceIdType.MESH).start()

    own.wait()
    most = out_ref.at[pl.ds(0, n_ep - 1)]
    pltpu.make_async_copy(most, most, send_sem).wait()
    pltpu.make_async_copy(most, most, recv_sem).wait()


def solution(mesh):
    n_ep = mesh.shape['ep']
    n_pp = mesh.shape['pp']
    tok_spec = P('pp', 'ep', None)
    dense_spec = P('pp', None, None)
    exp_spec = P('pp', 'ep', None, None)
    next_perm = [(stage, (stage + 1) % n_pp) for stage in range(n_pp)]
    prev_perm = [(stage, (stage - 1) % n_pp) for stage in range(n_pp)]

    def body(x_fwd, ids_fwd, gates_fwd, x_saved, grad_out, ids_bwd, gates_bwd, w_in, w_out, w_gate, w_up, w_down):
        x_fwd, x_saved, grad_out = x_fwd[0], x_saved[0], grad_out[0]
        w_in, w_out, w_gate, w_up, w_down = w_in[0], w_out[0], w_gate[0], w_up[0], w_down[0]
        tok, hid = x_fwd.shape
        ff = w_in.shape[1]
        n_exp = w_gate.shape[0] * n_ep
        eff = w_gate.shape[2]
        cap = 2 * tok // n_exp
        slots = n_exp * cap
        blk = min(256, tok)
        chunk = min(512, slots)
        cfg = (tok, n_exp, cap, blk, chunk)
        ids_f, ids_b = ids_fwd.reshape(1, tok), ids_bwd.reshape(1, tok)
        gate_f, gate_b = gates_fwd.reshape(1, tok).astype(F32), gates_bwd.reshape(1, tok).astype(F32)
        grouped = (2, n_ep, cap, hid)
        flat = (slots, hid)

        sz, sd, h_b, slot_b = vmem_call(
            functools.partial(pre_bwd_kernel, cfg),
            [(flat, BF16), (flat, BF16), ((tok, hid), BF16), ((1, tok), jnp.int32)],
            [pltpu.VMEM((tok, 2 * hid), BF16)], 11 * 10 ** 9,
        )(x_saved, grad_out, ids_b, gate_b, w_in, w_out)
        rz, rd = exchange(n_ep, 1, sz.reshape(grouped), sd.reshape(grouped))
        sf, h_f, slot_f = vmem_call(
            functools.partial(pre_fwd_kernel, cfg),
            [(flat, BF16), ((tok, hid), BF16), ((1, tok), jnp.int32)],
            [pltpu.VMEM((tok, hid), BF16)], 6 * 10 ** 9,
        )(x_fwd, ids_f, w_in, w_out)
        rf, = exchange(n_ep, 2, sf.reshape(grouped))
        dz, dw_gate, dw_up, dw_down = vmem_call(
            functools.partial(expert_bwd_kernel, blk),
            [(flat, BF16), (w_gate.shape, F32), (w_up.shape, F32), (w_down.shape, F32)],
            [pltpu.VMEM((hid, eff), F32)], 7 * 10 ** 9,
        )(rz.reshape(flat), rd.reshape(flat), w_gate, w_up, w_down)
        bz, = exchange(n_ep, 3, dz.reshape(grouped))
        of, = vmem_call(functools.partial(expert_fwd_kernel, blk), [(flat, BF16)], flops=3 * 10 ** 9)(
            rf.reshape(flat), w_gate, w_up, w_down)
        bf, = exchange(n_ep, 4, of.reshape(grouped))
        dx_out, dw_in, dw_out = vmem_call(
            functools.partial(post_bwd_kernel, blk),
            [((tok, hid), BF16), (w_in.shape, F32), (w_out.shape, F32)],
            [pltpu.VMEM((hid, ff), F32)], 9 * 10 ** 9,
        )(bz.reshape(flat), slot_b, h_b, grad_out, x_saved, w_in, w_out)
        y_out, = vmem_call(functools.partial(post_fwd_kernel, blk), [((tok, hid), BF16)], flops=4 * 10 ** 9)(
            bf.reshape(flat), slot_f, gate_f, h_f)
        y_next = lax.ppermute(y_out, 'pp', next_perm)
        dx_prev = lax.ppermute(dx_out, 'pp', prev_perm)

        lanes = 128
        piece = dw_in.size * 2 // n_ep // lanes
        both = jnp.concatenate([dw_in.reshape(-1, lanes), dw_out.reshape(-1, lanes)], axis=0).reshape(1, n_ep, piece, lanes)
        parts, = exchange(n_ep, 5, both)
        mine, = vmem_call(functools.partial(reduce_kernel, n_ep), [((piece, lanes), F32)])(parts)
        full = pl.pallas_call(
            functools.partial(spread_kernel, n_ep),
            out_shape=jax.ShapeDtypeStruct((n_ep, piece, lanes), F32),
            in_specs=[ANY], out_specs=ANY,
            scratch_shapes=[pltpu.SemaphoreType.DMA] * 3,
            compiler_params=pltpu.CompilerParams(collective_id=6, has_side_effects=True),
        )(mine)
        full = full.reshape(2, -1)
        dw_in, dw_out = full[0].reshape(w_in.shape), full[1].reshape(w_out.shape)
        return (y_next[None], dx_prev[None], dw_in[None], dw_out[None], dw_gate[None], dw_up[None], dw_down[None])

    return jax.shard_map(body, mesh=mesh,
                         in_specs=(tok_spec, tok_spec, tok_spec, tok_spec, tok_spec, tok_spec, tok_spec, dense_spec, dense_spec, exp_spec, exp_spec, exp_spec),
                         out_specs=(tok_spec, tok_spec, dense_spec, dense_spec, exp_spec, exp_spec, exp_spec),
                         check_vma=False)
```

time: 565 us -> 375 us (0.66); the launches traced: 555 us -> 374 us
  Pallas kernels: 0 us -> 339 us
  local copies, waits for them, and re-layouts: 222 us -> 29.9 us
  waiting for transfers between devices: 126 us -> 0.01 us
  other arithmetic: 84.7 us -> 2 us
  matrix products: 55.6 us -> 0 us
  starting transfers between devices: 50.8 us -> 2.97 us
  between operations: 15.4 us -> 0.9 us
    pallas_call x0 -> x13, Pallas kernels: none -> 339 us  [the longest x5 226 us: exchange(): pl.pallas_call(functools.partial(exchange_kernel, n_ep, n), out_shape=[ja...]
    gather x16 -> x0, local copies, waits for them, and re-layouts: 170 us -> none  [the longest x3 50.4 us: gather_rows(): picked = jnp.take(tok_rows, src_tok, axis=0)]
    psum x1 -> x0, waiting for transfers between devices: 113 us -> none  [body(): dw_in = lax.psum(dw_in, 'ep')]
    dot_general x17 -> x0, matrix products: 55.6 us -> none  [the longest x1 7.85 us: expert_backward(): jnp.einsum('emf,emd->efd', act_bf, grad_rows, preferred_element_type=jnp....]
    all_to_all x5 -> x0, starting transfers between devices: 50 us -> none  [the longest x1 12.4 us: body(): lax.all_to_all(gather_rows(z_fwd, tok_f, valid_f), 'ep', 0, 1, tiled=True)]
    scatter-add x2 -> x0, other arithmetic: 30 us -> none  [route_plan(): counts = jnp.bincount(flat_ids, length=num_exp)]
    convert_element_type x4 -> x0, local copies, waits for them, and re-layouts: 22.1 us -> none  [the longest x1 14.2 us: expert_backward(): return (grad_in.astype(jnp.bfloat16), dw_gate, dw_up, dw_down)]
    sort x4 -> x0, other arithmetic: 20.9 us -> none  [the longest x2 10.8 us: route_plan(): route_order = jnp.argsort(flat_ids, stable=True)]
  transfers between devices with their start and end apart: 8 -> 2, of which waited for: 4 -> 0; matrix products, arithmetic and copies ran while one was open for 43% -> 1% of each run, Pallas kernels for 0% -> 44%
where the time goes in v1:
time: 375 us; the launch traced here: 374 us
  Pallas kernels  339 us (90%)
  local copies, waits for them, and re-layouts  29.9 us (8%)
    pallas_call x5, Pallas kernels, exchange(): pl.pallas_call(functools.partial(exchange_kernel, n_ep, n), out_shape=[ja...  226 us
    pallas_call x1, Pallas kernels, body(): pl.pallas_call(functools.partial(spread_kernel, n_ep), out_shape=jax.Shap...  31.6 us
    unnamed x62, local copies, waits for them, and re-layouts  26.2 us
    pallas_call x1, Pallas kernels, body(): vmem_call(functools.partial(post_bwd_kernel, blk), [((tok, hid), BF16), (...  22.4 us
    pallas_call x1, Pallas kernels, body(): vmem_call(functools.partial(pre_bwd_kernel, cfg), [(flat, BF16), (flat, B...  16.8 us
    pallas_call x1, Pallas kernels, body(): vmem_call(functools.partial(expert_bwd_kernel, blk), [(flat, BF16), (w_ga...  16.5 us
    pallas_call x1, Pallas kernels, body(): vmem_call(functools.partial(pre_fwd_kernel, cfg), [(flat, BF16), ((tok, h...  11.1 us
  transfers between devices with their start and end apart: 2, of which 0 were waited for; matrix products, arithmetic and copies ran while one was open for 1% of the time, Pallas kernels for 44%

profile of v1, /device:TPU:1, one launch (start us, length us, event | category | flops | bytes accessed | tf_op | source)
XLA Modules:
  0.0 374.3 jit_solution(13983658940292921850)
XLA Ops:
  0.6 0.7 bitcast_convert_fusion.gate_ref
  1.3 0.0 copy-start.2
  1.4 1.2 copy-done.2
  2.6 1.2 copy-done.3
  3.8 1.0 copy-done.6
  4.8 1.0 copy-done.8
  5.8 0.7 copy-done.16
  6.5 16.8 %shard_map.176 = (bf16[4096,256]{1,0:T(8,128)(2,1)S(1)}, bf16[4096,256]{1,0:T(8,128)(2,1)}, bf16[2048,256]{1,0:T(8,128)(2,1)S(1)}, s32[1,2048]{1,0:T(1,128)S(1)}) custom-call(bf16[2048,256]{1,0:T(8,128)(2,1)S(1)} %bitcast.33, bf16[2048,256]{1,0:T(8,128)(2,1)S(1)} %bitcast.34, s32[1,2048]{1,0:T(1,128)S(1)} %bitcast.49, ...), custom_call_target="tpu_custom_call" | custom-call | flops 11000000512 | bytes 8388608 | tf_op jit(solution)/shard_map/pallas_call | solution.py:316
  23.3 1.3 copy-done.19
  24.6 1.0 copy-done.27
  25.6 73.0 %shard_map.177 = (bf16[2,64,32,256]{3,2,1,0:T(8,128)(2,1)}, bf16[2,64,32,256]{3,2,1,0:T(8,128)(2,1)}) custom-call(bf16[2,64,32,256]{3,2,1,0:T(8,128)(2,1)} %bitcast.52, bf16[2,64,32,256]{3,2,1,0:T(8,128)(2,1)} %bitcast.60), custom_call_target="tpu_custom_call" | custom-call | flops 10000000000 | bytes 8388608 | tf_op jit(solution)/shard_map/pallas_call | solution.py:254
  98.6 0.0 copy-done.10
  98.6 0.0 copy-done.12
  98.6 0.0 copy-done.14
  98.7 0.0 copy-start.18
  98.7 1.6 copy-done.18
  100.2 16.5 %shard_map.178 = (bf16[4096,256]{1,0:T(8,128)(2,1)S(1)}, f32[2,256,384]{2,1,0:T(8,128)}, f32[2,256,384]{2,1,0:T(8,128)}, f32[2,384,256]{2,1,0:T(8,128)}) custom-call(bf16[4096,256]{1,0:T(8,128)(2,1)S(1)} %bitcast.51, bf16[4096,256]{1,0:T(8,128)(2,1)} %bitcast.59, bf16[2,256,384]{2,1,0:T(8,128)(2,1)S(1)} %bitcast.43, bf16[2,256,384]{2,1,0:T(8,128)(2,1)S(1)} %bitcast.45, ...), custom_call_target="tpu_custom_call" | custom-call | flops 7000000000 | bytes 8388608 | tf_op jit(solution)/shard_map/pallas_call | solution.py:328
  116.7 1.4 copy-done.20
  118.1 45.8 %shard_map.179 = bf16[2,64,32,256]{3,2,1,0:T(8,128)(2,1)} custom-call(bf16[2,64,32,256]{3,2,1,0:T(8,128)(2,1)} %bitcast.53), custom_call_target="tpu_custom_call" | custom-call | flops 10000000000 | bytes 8388608 | tf_op jit(solution)/shard_map/pallas_call | solution.py:254
  163.9 0.0 copy-done.4
  163.9 0.0 copy-done.7
  163.9 0.0 copy-done.9
  163.9 0.0 copy-start.28
  163.9 1.2 copy-done.28
  165.2 22.4 %shard_map.180 = (bf16[2048,256]{1,0:T(8,128)(2,1)}, f32[256,768]{1,0:T(8,128)S(1)}, f32[768,256]{1,0:T(8,128)S(1)}) custom-call(bf16[4096,256]{1,0:T(8,128)(2,1)} %bitcast.61, s32[1,2048]{1,0:T(1,128)S(1)} %get-tuple-element.31.slot_ref, bf16[2048,256]{1,0:T(8,128)(2,1)S(1)} %copy-done.28, bf16[2048,256]{1,0:T(8,128)(2,1)S(1)} %bitcast.35, ...), custom_call_target="tpu_custom_call" | custom-call | flops 8999999488 | bytes 8388608 | tf_op jit(solution)/shard_map/pallas_call | solution.py:337
  187.6 1.3 collective-permute-start.1
  188.9 0.0 copy-done.5
  188.9 0.0 copy-done.17
  188.9 11.1 %shard_map.171 = (bf16[4096,256]{1,0:T(8,128)(2,1)S(1)}, bf16[2048,256]{1,0:T(8,128)(2,1)S(1)}, s32[1,2048]{1,0:T(1,128)S(1)}) custom-call(bf16[2048,256]{1,0:T(8,128)(2,1)S(1)} %bitcast.36, s32[1,2048]{1,0:T(1,128)S(1)} %bitcast.50, bf16[256,768]{1,0:T(8,128)(2,1)S(1)} %bitcast.39, bf16[768,256]{1,0:T(8,128)(2,1)S(1)} %bitcast.42), custom_call_target="tpu_custom_call" | custom-call | flops 6000000000 | bytes 8388608 | tf_op jit(solution)/shard_map/pallas_call | solution.py:322
  200.0 0.0 copy-start.22
  200.0 1.3 copy-done.22
  201.4 1.0 copy-done.25
  202.3 36.2 %shard_map.172 = bf16[2,64,32,256]{3,2,1,0:T(8,128)(2,1)} custom-call(bf16[2,64,32,256]{3,2,1,0:T(8,128)(2,1)} %bitcast.55), custom_call_target="tpu_custom_call" | custom-call | flops 10000000000 | bytes 8388608 | tf_op jit(solution)/shard_map/pallas_call | solution.py:254
  238.5 0.0 copy-done.11
  238.5 0.0 copy-done.13
  238.5 0.0 copy-done.15
  238.5 0.0 copy-start.23
  238.6 1.6 copy-done.23
  240.1 6.9 %shard_map.173 = bf16[4096,256]{1,0:T(8,128)(2,1)S(1)} custom-call(bf16[4096,256]{1,0:T(8,128)(2,1)S(1)} %bitcast.56, bf16[2,256,384]{2,1,0:T(8,128)(2,1)S(1)} %bitcast.44, bf16[2,256,384]{2,1,0:T(8,128)(2,1)S(1)} %bitcast.46, bf16[2,384,256]{2,1,0:T(8,128)(2,1)S(1)} %bitcast.48), custom_call_target="tpu_custom_call" | custom-call | flops 3000000000 | bytes 8388608 | tf_op jit(solution)/shard_map/pallas_call | solution.py:334
  247.0 0.0 copy-start.24
  247.0 1.3 copy-done.24
  248.4 39.5 %shard_map.174 = bf16[2,64,32,256]{3,2,1,0:T(8,128)(2,1)} custom-call(bf16[2,64,32,256]{3,2,1,0:T(8,128)(2,1)} %bitcast.57), custom_call_target="tpu_custom_call" | custom-call | flops 10000000000 | bytes 8388608 | tf_op jit(solution)/shard_map/pallas_call | solution.py:254
  287.8 0.0 copy-done.29
  287.9 0.0 copy-start.21
  287.9 1.6 copy-done.21
  289.4 1.2 copy-done.26
  290.7 7.3 %shard_map.175 = bf16[2048,256]{1,0:T(8,128)(2,1)S(1)} custom-call(bf16[4096,256]{1,0:T(8,128)(2,1)S(1)} %bitcast.54, s32[1,2048]{1,0:T(1,128)S(1)} %get-tuple-element.24.slot_ref, f32[1,2048]{1,0:T(1,128)S(1)} %bitcast_convert_fusion.1.gate_ref, bf16[2048,256]{1,0:T(8,128)(2,1)S(1)} %copy-done.26), custom_call_target="tpu_custom_call" | custom-call | flops 4000000000 | bytes 8388608 | tf_op jit(solution)/shard_map/pallas_call | solution.py:342
  298.0 1.7 collective-permute-start
  299.7 0.1 reshape.106
  299.7 0.1 reshape.107
  299.8 1.3 pad_maximum_fusion
  301.1 31.4 %shard_map.181.part_ref = f32[1,64,48,128]{3,2,1,0:T(8,128)} custom-call(f32[1,64,48,128]{3,2,1,0:T(8,128)} %bitcast.58), custom_call_target="tpu_custom_call" | custom-call | flops 10000000000 | bytes 8388608 | tf_op jit(solution)/shard_map/pallas_call | solution.py:254
  332.5 0.0 copy-start
  332.5 1.4 copy-done
  333.9 0.1 shard_map.182.piece_ref
  334.0 0.6 copy-done.1
  334.6 31.6 %shard_map.183 = f32[64,48,128]{2,1,0:T(8,128)} custom-call(f32[48,128]{1,0:T(8,128)} %copy-done.1), custom_call_target="tpu_custom_call" | custom-call | tf_op jit(solution)/shard_map/pallas_call | solution.py:352
  366.2 1.5 fusion
  367.7 1.0 broadcast_in_dim_reshape_squeeze.6
  368.7 1.1 broadcast_in_dim_reshape_squeeze.7
  369.8 0.0 collective-permute-done.1
  369.8 0.0 collective-permute-done
  369.8 2.3 copy.21
  372.1 2.3 copy.22
  (23 shorter events, 0.0 us)
Async XLA Ops:
  1.3 1.2 copy-start.2
  2.6 1.2 copy-start.3
  3.8 1.0 copy-start.6
  4.8 1.0 copy-start.8
  5.8 0.7 copy-start.16
  23.3 1.3 copy-start.19
  24.6 1.0 copy-start.27
  25.6 73.0 %copy-start.10 = (bf16[1,2,256,384]{3,2,1,0:T(8,128)(2,1)S(1)}, bf16[1,2,256,384]{3,2,1,0:T(8,128)(2,1)}, u32[]{:S(2)}) copy-start(bf16[1,2,256,384]{3,2,1,0:T(8,128)(2,1)} %param.21) | copy-start | bytes 1179652
  25.6 73.1 %copy-start.12 = (bf16[1,2,256,384]{3,2,1,0:T(8,128)(2,1)S(1)}, bf16[1,2,256,384]{3,2,1,0:T(8,128)(2,1)}, u32[]{:S(2)}) copy-start(bf16[1,2,256,384]{3,2,1,0:T(8,128)(2,1)} %param.22) | copy-start | bytes 1179652
  25.6 73.1 %copy-start.14 = (bf16[1,2,384,256]{3,2,1,0:T(8,128)(2,1)S(1)}, bf16[1,2,384,256]{3,2,1,0:T(8,128)(2,1)}, u32[]{:S(2)}) copy-start(bf16[1,2,384,256]{3,2,1,0:T(8,128)(2,1)} %param.23) | copy-start | bytes 1179652
  98.7 1.6 copy-start.18
  116.7 1.4 copy-start.20
  118.1 45.8 %copy-start.4 = (bf16[1,2048,256]{2,1,0:T(8,128)(2,1)S(1)}, bf16[1,2048,256]{2,1,0:T(8,128)(2,1)}, u32[]{:S(2)}) copy-start(bf16[1,2048,256]{2,1,0:T(8,128)(2,1)} %param.16) | copy-start | bytes 3145732
  118.1 45.8 %copy-start.7 = (bf16[1,256,768]{2,1,0:T(8,128)(2,1)S(1)}, bf16[1,256,768]{2,1,0:T(8,128)(2,1)}, u32[]{:S(2)}) copy-start(bf16[1,256,768]{2,1,0:T(8,128)(2,1)} %param.19) | copy-start | bytes 1179652
  118.1 45.8 %copy-start.9 = (bf16[1,768,256]{2,1,0:T(8,128)(2,1)S(1)}, bf16[1,768,256]{2,1,0:T(8,128)(2,1)}, u32[]{:S(2)}) copy-start(bf16[1,768,256]{2,1,0:T(8,128)(2,1)} %param.20) | copy-start | bytes 1179652
  163.9 1.2 copy-start.28
  165.2 23.7 %copy-start.5 = (bf16[1,2048,256]{2,1,0:T(8,128)(2,1)S(1)}, bf16[1,2048,256]{2,1,0:T(8,128)(2,1)}, u32[]{:S(2)}) copy-start(bf16[1,2048,256]{2,1,0:T(8,128)(2,1)} %param.12) | copy-start | bytes 3145732
  165.2 23.7 %copy-start.17 = (s32[1,2048,1]{1,2,0:T(1,128)S(1)}, s32[1,2048,1]{1,2,0:T(1,128)}, u32[]{:S(2)}) copy-start(s32[1,2048,1]{1,2,0:T(1,128)} %param.13) | copy-start | bytes 24580
  187.6 182.2 %collective-permute-start.1 = (bf16[2048,256]{1,0:T(8,128)(2,1)}, bf16[2048,256]{1,0:T(8,128)(2,1)}, u32[]{:S(2)}, u32[]{:S(2)}) collective-permute-start(bf16[2048,256]{1,0:T(8,128)(2,1)} %get-tuple-element.33), channel_id=1, source_target_pairs={{0,64},{64,0},{1,65},{65,1},{2,66},{66,2},{3,67},{67,3},{4,68},{68... | collective-permute-start | bytes 3145736 | tf_op jit(solution)/shard_map/ppermute | solution.py:345
  200.0 1.4 copy-start.22
  201.4 1.0 copy-start.25
  202.3 36.2 %copy-start.11 = (bf16[1,2,256,384]{3,2,1,0:T(8,128)(2,1)S(1)}, bf16[1,2,256,384]{3,2,1,0:T(8,128)(2,1)}, u32[]{:S(2)}) copy-start(bf16[1,2,256,384]{3,2,1,0:T(8,128)(2,1)} %param.21) | copy-start | bytes 1179652
  202.3 36.2 %copy-start.13 = (bf16[1,2,256,384]{3,2,1,0:T(8,128)(2,1)S(1)}, bf16[1,2,256,384]{3,2,1,0:T(8,128)(2,1)}, u32[]{:S(2)}) copy-start(bf16[1,2,256,384]{3,2,1,0:T(8,128)(2,1)} %param.22) | copy-start | bytes 1179652
  202.3 36.2 %copy-start.15 = (bf16[1,2,384,256]{3,2,1,0:T(8,128)(2,1)S(1)}, bf16[1,2,384,256]{3,2,1,0:T(8,128)(2,1)}, u32[]{:S(2)}) copy-start(bf16[1,2,384,256]{3,2,1,0:T(8,128)(2,1)} %param.23) | copy-start | bytes 1179652
  238.5 1.6 copy-start.23
  247.0 1.4 copy-start.24
  248.4 39.5 %copy-start.29 = (bf16[1,2048,1]{1,2,0:T(2,128)(2,1)S(1)}, bf16[1,2048,1]{1,2,0:T(2,128)(2,1)}, u32[]{:S(2)}) copy-start(bf16[1,2048,1]{1,2,0:T(2,128)(2,1)} %param.14) | copy-start | bytes 12292
  287.9 1.6 copy-start.21
  289.4 1.2 copy-start.26
  298.0 71.8 %collective-permute-start = (bf16[2048,256]{1,0:T(8,128)(2,1)S(1)}, bf16[2048,256]{1,0:T(8,128)(2,1)}, u32[]{:S(2)}, u32[]{:S(2)}) collective-permute-start(bf16[2048,256]{1,0:T(8,128)(2,1)S(1)} %shard_map.175), channel_id=1, source_target_pairs={{0,64},{64,0},{1,65},{65,1},{2,66},{66,2},{3,67},{67,3},{4,68},{68... | collective-permute-start | bytes 3145736 | tf_op jit(solution)/shard_map/ppermute | solution.py:344
  332.5 1.4 copy-start
  334.0 0.6 copy-start.1

commit v2 on v1

--- a/solution.py
+++ b/solution.py
@@ -227,39 +227,69 @@
     return (z * side + y) * side + x
 
 
-def exchange_kernel(n_ep, n, *refs):
-    ins, outs = refs[:n], refs[n:2 * n]
-    send_sem, recv_sem, local_sem = refs[2 * n:]
+def relays(n_ep):
+    if n_ep != 64:
+        return [[], [], []]
+    rest = [(a, b) for a in (0, 1, 3) for b in (0, 1, 3)][1:]
+    offs = [[(2, a, b) for a, b in rest], [(a, 2, b) for a, b in rest], [(a, b, 2) for a, b in rest]]
+    return [[x + 4 * y + 16 * z for x, y, z in g] for g in offs]
+
+
+def exchange_kernel(n_ep, n, side, *refs):
+    ins, outs, mid = refs[:n], refs[n:2 * n], refs[2 * n:3 * n]
+    send_sem, recv_sem, local_sem, relay_sem, fwd_sem = refs[3 * n:]
     me = enter(n_ep)
+    groups = relays(n_ep)
+    via = sum(groups, [])
     for i in range(n):
         pltpu.make_async_copy(ins[i].at[:, me], outs[i].at[:, me], local_sem.at[i]).start()
 
-    @pl.loop(1, n_ep)
-    def _(k):
+    def send(src, dst, s_sem, r_sem, to):
+        pltpu.make_async_remote_copy(src, dst, s_sem, r_sem, device_id={'ep': to}, device_id_type=pl.DeviceIdType.MESH).start()
+
+    for j in range(len(via) // 3):
+        for axis, group in enumerate(groups):
+            hop = peer(me, side * 4 ** axis, n_ep)
+            to = peer(me, group[j], n_ep)
+            for i in range(n):
+                send(ins[i].at[:, to], mid[i].at[axis, :, j], send_sem.at[i], relay_sem.at[i, axis], hop)
+    for k in range(1, n_ep):
+        if k in via:
+            continue
         to = peer(me, k, n_ep)
         for i in range(n):
-            pltpu.make_async_remote_copy(
-                ins[i].at[:, to], outs[i].at[:, me], send_sem.at[i], recv_sem.at[i],
-                device_id={'ep': to}, device_id_type=pl.DeviceIdType.MESH).start()
+            send(ins[i].at[:, to], outs[i].at[:, me], send_sem.at[i], recv_sem.at[i], to)
+    if via:
+        for i in range(n):
+            for axis, group in enumerate(groups):
+                pltpu.make_async_copy(mid[i].at[axis], mid[i].at[axis], relay_sem.at[i, axis]).wait()
+                origin = peer(me, (4 - side) * 4 ** axis, n_ep)
+                for j, k in enumerate(group):
+                    send(mid[i].at[axis, :, j], outs[i].at[:, origin], fwd_sem.at[i], recv_sem.at[i], peer(origin, k, n_ep))
 
     for i in range(n):
         pltpu.make_async_copy(ins[i].at[:, me], outs[i].at[:, me], local_sem.at[i]).wait()
         most = pl.ds(0, n_ep - 1)
         pltpu.make_async_copy(ins[i].at[:, most], ins[i].at[:, most], send_sem.at[i]).wait()
         pltpu.make_async_copy(outs[i].at[:, most], outs[i].at[:, most], recv_sem.at[i]).wait()
-
-
-def exchange(n_ep, cid, *bufs):
+        if via:
+            pltpu.make_async_copy(mid[i], mid[i], fwd_sem.at[i]).wait()
+
+
+def exchange(n_ep, cid, *bufs, side=3):
     n = len(bufs)
+    rows = max(1, len(relays(n_ep)[0]))
+    mids = [jax.ShapeDtypeStruct((3, b.shape[0], rows, *b.shape[2:]), b.dtype) for b in bufs]
+    dma = pltpu.SemaphoreType.DMA
     return pl.pallas_call(
-        functools.partial(exchange_kernel, n_ep, n),
-        out_shape=[jax.ShapeDtypeStruct(b.shape, b.dtype) for b in bufs],
+        functools.partial(exchange_kernel, n_ep, n, side),
+        out_shape=[jax.ShapeDtypeStruct(b.shape, b.dtype) for b in bufs] + mids,
         in_specs=[ANY] * n,
-        out_specs=[ANY] * n,
-        scratch_shapes=[pltpu.SemaphoreType.DMA((n,)), pltpu.SemaphoreType.DMA((n,)), pltpu.SemaphoreType.DMA((n,))],
+        out_specs=[ANY] * (2 * n),
+        scratch_shapes=[dma((n,)), dma((n,)), dma((n,)), dma((n, 3)), dma((n,))],
         compiler_params=pltpu.CompilerParams(collective_id=cid, has_side_effects=True),
         cost_estimate=pl.CostEstimate(flops=10 ** 10, bytes_accessed=8 * MIB, transcendentals=0),
-    )(*bufs)
+    )(*bufs)[:n]
 
 
 def reduce_kernel(n_ep, part_ref, sum_ref):
@@ -324,7 +354,7 @@
             [(flat, BF16), ((tok, hid), BF16), ((1, tok), jnp.int32)],
             [pltpu.VMEM((tok, hid), BF16)], 6 * 10 ** 9,
         )(x_fwd, ids_f, w_in, w_out)
-        rf, = exchange(n_ep, 2, sf.reshape(grouped))
+        rf, = exchange(n_ep, 2, sf.reshape(grouped), side=1)
         dz, dw_gate, dw_up, dw_down = vmem_call(
             functools.partial(expert_bwd_kernel, blk),
             [(flat, BF16), (w_gate.shape, F32), (w_up.shape, F32), (w_down.shape, F32)],

time: 375 us -> 380 us (1.013)
  Pallas kernels: 339 us -> 345 us
    pallas_call x5, Pallas kernels: 226 us -> 233 us  [exchange(): pl.pallas_call(functools.partial(exchange_kernel, n_ep, n, side), out_sha...]
  transfers between devices with their start and end apart: 2 -> 2, of which waited for: 0 -> 0; matrix products, arithmetic and copies ran while one was open for 1% -> 1% of each run, Pallas kernels for 44% -> 45%
where the time goes in v2:
time: 380 us; the launch traced here: 378 us
  Pallas kernels  345 us (91%)
  local copies, waits for them, and re-layouts  29.9 us (8%)
    pallas_call x5, Pallas kernels, exchange(): pl.pallas_call(functools.partial(exchange_kernel, n_ep, n, side), out_sha...  233 us
    pallas_call x1, Pallas kernels, body(): pl.pallas_call(functools.partial(spread_kernel, n_ep), out_shape=jax.Shap...  30.5 us
    unnamed x62, local copies, waits for them, and re-layouts  26.2 us
    pallas_call x1, Pallas kernels, body(): vmem_call(functools.partial(post_bwd_kernel, blk), [((tok, hid), BF16), (...  22.5 us
    pallas_call x1, Pallas kernels, body(): vmem_call(functools.partial(pre_bwd_kernel, cfg), [(flat, BF16), (flat, B...  16.8 us
    pallas_call x1, Pallas kernels, body(): vmem_call(functools.partial(expert_bwd_kernel, blk), [(flat, BF16), (w_ga...  16.4 us
    pallas_call x1, Pallas kernels, body(): vmem_call(functools.partial(pre_fwd_kernel, cfg), [(flat, BF16), ((tok, h...  11.2 us
  transfers between devices with their start and end apart: 2, of which 0 were waited for; matrix products, arithmetic and copies ran while one was open for 1% of the time, Pallas kernels for 45%

profile of v2, /device:TPU:1, one launch (start us, length us, event | category | flops | bytes accessed | tf_op | source)
XLA Modules:
  0.0 378.1 jit_solution(12069894815071453299)
XLA Ops:
  0.6 0.7 bitcast_convert_fusion.gate_ref
  1.3 0.0 copy-start.2
  1.4 1.2 copy-done.2
  2.6 1.2 copy-done.3
  3.8 1.0 copy-done.6
  4.8 1.0 copy-done.8
  5.8 0.7 copy-done.16
  6.5 16.8 %shard_map.176 = (bf16[4096,256]{1,0:T(8,128)(2,1)S(1)}, bf16[4096,256]{1,0:T(8,128)(2,1)}, bf16[2048,256]{1,0:T(8,128)(2,1)S(1)}, s32[1,2048]{1,0:T(1,128)S(1)}) custom-call(bf16[2048,256]{1,0:T(8,128)(2,1)S(1)} %bitcast.33, bf16[2048,256]{1,0:T(8,128)(2,1)S(1)} %bitcast.34, s32[1,2048]{1,0:T(1,128)S(1)} %bitcast.49, ...), custom_call_target="tpu_custom_call" | custom-call | flops 11000000512 | bytes 8388608 | tf_op jit(solution)/shard_map/pallas_call | solution.py:346
  23.3 1.3 copy-done.19
  24.6 1.0 copy-done.27
  25.6 82.6 %shard_map.177 = (bf16[2,64,32,256]{3,2,1,0:T(8,128)(2,1)}, bf16[2,64,32,256]{3,2,1,0:T(8,128)(2,1)}, bf16[3,2,8,32,256]{4,3,2,1,0:T(8,128)(2,1)}, bf16[3,2,8,32,256]{4,3,2,1,0:T(8,128)(2,1)}) custom-call(bf16[2,64,32,256]{3,2,1,0:T(8,128)(2,1)} %bitcast.52, bf16[2,64,32,256]{3,2,1,0:T(8,128)(2,1)} %bitcast.60), custom_call_target="tpu_custom_call" | custom-call | flops 10000000000 | bytes 8388608 | tf_op jit(solution)/shard_map/pallas_call | solution.py:284
  108.2 0.0 copy-done.10
  108.2 0.0 copy-done.12
  108.2 0.0 copy-done.14
  108.2 0.0 copy-start.18
  108.2 1.6 copy-done.18
  109.8 16.4 %shard_map.178 = (bf16[4096,256]{1,0:T(8,128)(2,1)S(1)}, f32[2,256,384]{2,1,0:T(8,128)}, f32[2,256,384]{2,1,0:T(8,128)}, f32[2,384,256]{2,1,0:T(8,128)}) custom-call(bf16[4096,256]{1,0:T(8,128)(2,1)S(1)} %bitcast.51, bf16[4096,256]{1,0:T(8,128)(2,1)} %bitcast.59, bf16[2,256,384]{2,1,0:T(8,128)(2,1)S(1)} %bitcast.43, bf16[2,256,384]{2,1,0:T(8,128)(2,1)S(1)} %bitcast.45, ...), custom_call_target="tpu_custom_call" | custom-call | flops 7000000000 | bytes 8388608 | tf_op jit(solution)/shard_map/pallas_call | solution.py:358
  126.2 1.4 copy-done.20
  127.6 36.3 %shard_map.179 = (bf16[2,64,32,256]{3,2,1,0:T(8,128)(2,1)}, bf16[3,2,8,32,256]{4,3,2,1,0:T(8,128)(2,1)}) custom-call(bf16[2,64,32,256]{3,2,1,0:T(8,128)(2,1)} %bitcast.53), custom_call_target="tpu_custom_call" | custom-call | flops 10000000000 | bytes 8388608 | tf_op jit(solution)/shard_map/pallas_call | solution.py:284
  163.9 0.0 copy-done.4
  163.9 0.0 copy-done.7
  163.9 0.0 copy-done.9
  164.0 0.0 copy-start.28
  164.0 1.2 copy-done.28
  165.2 22.5 %shard_map.180 = (bf16[2048,256]{1,0:T(8,128)(2,1)}, f32[256,768]{1,0:T(8,128)S(1)}, f32[768,256]{1,0:T(8,128)S(1)}) custom-call(bf16[4096,256]{1,0:T(8,128)(2,1)} %bitcast.61, s32[1,2048]{1,0:T(1,128)S(1)} %get-tuple-element.38.slot_ref, bf16[2048,256]{1,0:T(8,128)(2,1)S(1)} %copy-done.28, bf16[2048,256]{1,0:T(8,128)(2,1)S(1)} %bitcast.35, ...), custom_call_target="tpu_custom_call" | custom-call | flops 8999999488 | bytes 8388608 | tf_op jit(solution)/shard_map/pallas_call | solution.py:367
  187.6 0.4 collective-permute-start.1
  188.0 0.0 copy-done.5
  188.0 0.0 copy-done.17
  188.0 11.2 %shard_map.171 = (bf16[4096,256]{1,0:T(8,128)(2,1)S(1)}, bf16[2048,256]{1,0:T(8,128)(2,1)S(1)}, s32[1,2048]{1,0:T(1,128)S(1)}) custom-call(bf16[2048,256]{1,0:T(8,128)(2,1)S(1)} %bitcast.36, s32[1,2048]{1,0:T(1,128)S(1)} %bitcast.50, bf16[256,768]{1,0:T(8,128)(2,1)S(1)} %bitcast.39, bf16[768,256]{1,0:T(8,128)(2,1)S(1)} %bitcast.42), custom_call_target="tpu_custom_call" | custom-call | flops 6000000000 | bytes 8388608 | tf_op jit(solution)/shard_map/pallas_call | solution.py:352
  199.2 0.0 copy-start.22
  199.2 1.3 copy-done.22
  200.5 1.0 copy-done.25
  201.5 42.4 %shard_map.172 = (bf16[2,64,32,256]{3,2,1,0:T(8,128)(2,1)}, bf16[3,2,8,32,256]{4,3,2,1,0:T(8,128)(2,1)}) custom-call(bf16[2,64,32,256]{3,2,1,0:T(8,128)(2,1)} %bitcast.55), custom_call_target="tpu_custom_call" | custom-call | flops 10000000000 | bytes 8388608 | tf_op jit(solution)/shard_map/pallas_call | solution.py:284
  243.9 0.0 copy-done.11
  243.9 0.0 copy-done.13
  243.9 0.0 copy-done.15
  243.9 0.0 copy-start.23
  243.9 1.6 copy-done.23
  245.5 6.9 %shard_map.173 = bf16[4096,256]{1,0:T(8,128)(2,1)S(1)} custom-call(bf16[4096,256]{1,0:T(8,128)(2,1)S(1)} %bitcast.56, bf16[2,256,384]{2,1,0:T(8,128)(2,1)S(1)} %bitcast.44, bf16[2,256,384]{2,1,0:T(8,128)(2,1)S(1)} %bitcast.46, bf16[2,384,256]{2,1,0:T(8,128)(2,1)S(1)} %bitcast.48), custom_call_target="tpu_custom_call" | custom-call | flops 3000000000 | bytes 8388608 | tf_op jit(solution)/shard_map/pallas_call | solution.py:364
  252.4 0.0 copy-start.24
  252.4 1.3 copy-done.24
  253.7 37.2 %shard_map.174 = (bf16[2,64,32,256]{3,2,1,0:T(8,128)(2,1)}, bf16[3,2,8,32,256]{4,3,2,1,0:T(8,128)(2,1)}) custom-call(bf16[2,64,32,256]{3,2,1,0:T(8,128)(2,1)} %bitcast.57), custom_call_target="tpu_custom_call" | custom-call | flops 10000000000 | bytes 8388608 | tf_op jit(solution)/shard_map/pallas_call | solution.py:284
  290.9 0.0 copy-done.29
  291.0 0.0 copy-start.21
  291.0 1.6 copy-done.21
  292.6 1.2 copy-done.26
  293.8 7.3 %shard_map.175 = bf16[2048,256]{1,0:T(8,128)(2,1)S(1)} custom-call(bf16[4096,256]{1,0:T(8,128)(2,1)S(1)} %bitcast.54, s32[1,2048]{1,0:T(1,128)S(1)} %get-tuple-element.30.slot_ref, f32[1,2048]{1,0:T(1,128)S(1)} %bitcast_convert_fusion.1.gate_ref, bf16[2048,256]{1,0:T(8,128)(2,1)S(1)} %copy-done.26), custom_call_target="tpu_custom_call" | custom-call | flops 4000000000 | bytes 8388608 | tf_op jit(solution)/shard_map/pallas_call | solution.py:372
  301.1 0.3 collective-permute-start
  301.4 0.1 reshape.106
  301.5 0.1 reshape.107
  301.5 1.3 pad_maximum_fusion
  302.8 34.6 %shard_map.181 = (f32[1,64,48,128]{3,2,1,0:T(8,128)}, f32[3,1,8,48,128]{4,3,2,1,0:T(8,128)}) custom-call(f32[1,64,48,128]{3,2,1,0:T(8,128)} %bitcast.58), custom_call_target="tpu_custom_call" | custom-call | flops 10000000000 | bytes 8388608 | tf_op jit(solution)/shard_map/pallas_call | solution.py:284
  337.4 0.0 copy-start
  337.4 1.4 copy-done
  338.8 0.1 shard_map.182.piece_ref
  338.9 0.6 copy-done.1
  339.5 30.5 %shard_map.183 = f32[64,48,128]{2,1,0:T(8,128)} custom-call(f32[48,128]{1,0:T(8,128)} %copy-done.1), custom_call_target="tpu_custom_call" | custom-call | tf_op jit(solution)/shard_map/pallas_call | solution.py:382
  370.0 1.5 fusion
  371.5 1.0 broadcast_in_dim_reshape_squeeze.6
  372.5 1.1 broadcast_in_dim_reshape_squeeze.7
  373.6 0.0 collective-permute-done.1
  373.6 0.0 collective-permute-done
  373.6 2.3 copy.21
  375.9 2.3 copy.22
  (23 shorter events, 0.0 us)
Async XLA Ops:
  1.3 1.2 copy-start.2
  2.6 1.2 copy-start.3
  3.8 1.0 copy-start.6
  4.8 1.0 copy-start.8
  5.8 0.7 copy-start.16
  23.3 1.3 copy-start.19
  24.6 1.0 copy-start.27
  25.6 82.6 %copy-start.10 = (bf16[1,2,256,384]{3,2,1,0:T(8,128)(2,1)S(1)}, bf16[1,2,256,384]{3,2,1,0:T(8,128)(2,1)}, u32[]{:S(2)}) copy-start(bf16[1,2,256,384]{3,2,1,0:T(8,128)(2,1)} %param.21) | copy-start | bytes 1179652
  25.6 82.6 %copy-start.12 = (bf16[1,2,256,384]{3,2,1,0:T(8,128)(2,1)S(1)}, bf16[1,2,256,384]{3,2,1,0:T(8,128)(2,1)}, u32[]{:S(2)}) copy-start(bf16[1,2,256,384]{3,2,1,0:T(8,128)(2,1)} %param.22) | copy-start | bytes 1179652
  25.6 82.6 %copy-start.14 = (bf16[1,2,384,256]{3,2,1,0:T(8,128)(2,1)S(1)}, bf16[1,2,384,256]{3,2,1,0:T(8,128)(2,1)}, u32[]{:S(2)}) copy-start(bf16[1,2,384,256]{3,2,1,0:T(8,128)(2,1)} %param.23) | copy-start | bytes 1179652
  108.2 1.6 copy-start.18
  126.2 1.4 copy-start.20
  127.6 36.4 %copy-start.4 = (bf16[1,2048,256]{2,1,0:T(8,128)(2,1)S(1)}, bf16[1,2048,256]{2,1,0:T(8,128)(2,1)}, u32[]{:S(2)}) copy-start(bf16[1,2048,256]{2,1,0:T(8,128)(2,1)} %param.16) | copy-start | bytes 3145732
  127.6 36.4 %copy-start.7 = (bf16[1,256,768]{2,1,0:T(8,128)(2,1)S(1)}, bf16[1,256,768]{2,1,0:T(8,128)(2,1)}, u32[]{:S(2)}) copy-start(bf16[1,256,768]{2,1,0:T(8,128)(2,1)} %param.19) | copy-start | bytes 1179652
  127.6 36.4 %copy-start.9 = (bf16[1,768,256]{2,1,0:T(8,128)(2,1)S(1)}, bf16[1,768,256]{2,1,0:T(8,128)(2,1)}, u32[]{:S(2)}) copy-start(bf16[1,768,256]{2,1,0:T(8,128)(2,1)} %param.20) | copy-start | bytes 1179652
  164.0 1.2 copy-start.28
  165.2 22.8 %copy-start.5 = (bf16[1,2048,256]{2,1,0:T(8,128)(2,1)S(1)}, bf16[1,2048,256]{2,1,0:T(8,128)(2,1)}, u32[]{:S(2)}) copy-start(bf16[1,2048,256]{2,1,0:T(8,128)(2,1)} %param.12) | copy-start | bytes 3145732
  165.2 22.8 %copy-start.17 = (s32[1,2048,1]{1,2,0:T(1,128)S(1)}, s32[1,2048,1]{1,2,0:T(1,128)}, u32[]{:S(2)}) copy-start(s32[1,2048,1]{1,2,0:T(1,128)} %param.13) | copy-start | bytes 24580
  187.6 186.0 %collective-permute-start.1 = (bf16[2048,256]{1,0:T(8,128)(2,1)}, bf16[2048,256]{1,0:T(8,128)(2,1)}, u32[]{:S(2)}, u32[]{:S(2)}) collective-permute-start(bf16[2048,256]{1,0:T(8,128)(2,1)} %get-tuple-element.40), channel_id=1, source_target_pairs={{0,64},{64,0},{1,65},{65,1},{2,66},{66,2},{3,67},{67,3},{4,68},{68... | collective-permute-start | bytes 3145736 | tf_op jit(solution)/shard_map/ppermute | solution.py:375
  199.2 1.4 copy-start.22
  200.5 1.0 copy-start.25
  201.5 42.4 %copy-start.11 = (bf16[1,2,256,384]{3,2,1,0:T(8,128)(2,1)S(1)}, bf16[1,2,256,384]{3,2,1,0:T(8,128)(2,1)}, u32[]{:S(2)}) copy-start(bf16[1,2,256,384]{3,2,1,0:T(8,128)(2,1)} %param.21) | copy-start | bytes 1179652
  201.5 42.4 %copy-start.13 = (bf16[1,2,256,384]{3,2,1,0:T(8,128)(2,1)S(1)}, bf16[1,2,256,384]{3,2,1,0:T(8,128)(2,1)}, u32[]{:S(2)}) copy-start(bf16[1,2,256,384]{3,2,1,0:T(8,128)(2,1)} %param.22) | copy-start | bytes 1179652
  201.5 42.4 %copy-start.15 = (bf16[1,2,384,256]{3,2,1,0:T(8,128)(2,1)S(1)}, bf16[1,2,384,256]{3,2,1,0:T(8,128)(2,1)}, u32[]{:S(2)}) copy-start(bf16[1,2,384,256]{3,2,1,0:T(8,128)(2,1)} %param.23) | copy-start | bytes 1179652
  243.9 1.6 copy-start.23
  252.4 1.4 copy-start.24
  253.7 37.2 %copy-start.29 = (bf16[1,2048,1]{1,2,0:T(2,128)(2,1)S(1)}, bf16[1,2048,1]{1,2,0:T(2,128)(2,1)}, u32[]{:S(2)}) copy-start(bf16[1,2048,1]{1,2,0:T(2,128)(2,1)} %param.14) | copy-start | bytes 12292
  291.0 1.6 copy-start.21
  292.5 1.2 copy-start.26
  301.1 72.5 %collective-permute-start = (bf16[2048,256]{1,0:T(8,128)(2,1)S(1)}, bf16[2048,256]{1,0:T(8,128)(2,1)}, u32[]{:S(2)}, u32[]{:S(2)}) collective-permute-start(bf16[2048,256]{1,0:T(8,128)(2,1)S(1)} %shard_map.175), channel_id=1, source_target_pairs={{0,64},{64,0},{1,65},{65,1},{2,66},{66,2},{3,67},{67,3},{4,68},{68... | collective-permute-start | bytes 3145736 | tf_op jit(solution)/shard_map/ppermute | solution.py:374
  337.4 1.4 copy-start
  338.9 0.6 copy-start.1

commit v3 on v0

v3 whole, which is shorter than its diff:
```python
import functools

import jax
import jax.numpy as jnp
from jax import lax
from jax.experimental import pallas as pl
from jax.experimental.pallas import tpu as pltpu
from jax.sharding import PartitionSpec as P

EPS = 1e-6
F32 = jnp.float32
BF16 = jnp.bfloat16
MIB = 1024 * 1024
MESH = pl.DeviceIdType.MESH
ANY = pl.BlockSpec(memory_space=pl.ANY)
VMEM = pl.BlockSpec(memory_space=pltpu.VMEM)


def mm(a, b):
    return lax.dot_general(a, b, (((1,), (0,)), ((), ())), preferred_element_type=F32)


def mm_nt(a, b):
    return lax.dot_general(a, b, (((1,), (1,)), ((), ())), preferred_element_type=F32)


def mm_tn(a, b):
    return lax.dot_general(a, b, (((0,), (0,)), ((), ())), preferred_element_type=F32)


def inv_rms(v):
    return lax.rsqrt(jnp.mean(v * v, axis=-1, keepdims=True) + EPS)


def rms_vjp(v, inv, g):
    return inv * g - v * (inv * inv * inv) * jnp.mean(g * v, axis=-1, keepdims=True)


def plan(ids_ref, slot_ref, n_exp, cap, blk):
    tok = ids_ref.shape[1]
    upper = (lax.broadcasted_iota(jnp.int32, (blk, blk), 0) < lax.broadcasted_iota(jnp.int32, (blk, blk), 1))
    upper = jnp.where(upper, 1.0, 0.0).astype(BF16)
    expert = lax.broadcasted_iota(jnp.int32, (n_exp, blk), 0)
    carry = jnp.zeros((n_exp, 1), F32)
    for b in range(tok // blk):
        ids = ids_ref[:, b * blk:(b + 1) * blk]
        hot = jnp.where(expert == ids, 1.0, 0.0)
        before = mm(hot.astype(BF16), upper) + carry
        rank = jnp.sum(hot * before, axis=0, keepdims=True).astype(jnp.int32)
        carry = carry + jnp.sum(hot, axis=1, keepdims=True)
        slot_ref[:, b * blk:(b + 1) * blk] = (ids & 1) * (n_exp // 2 * cap) + (ids >> 1) * cap + rank


def column(row):
    n = row.shape[1]
    return jnp.transpose(jnp.broadcast_to(row, (128, n)))[:, :1]


def dense_tile(x, w_in, w_out):
    inv = inv_rms(x)
    normed = (x * inv).astype(BF16)
    pre = mm(normed, w_in)
    hid = (pre * jax.nn.sigmoid(pre)).astype(BF16)
    h = (x + mm(hid, w_out)).astype(BF16)
    return h


def dispatch(slot_ref, rows_ref, send_ref, size):
    tok = slot_ref.shape[1]
    half = send_ref.shape[1]
    for j in range(2):
        @pl.loop(0, half // size)
        def _(c):
            start = pl.multiple_of(c * size, size)
            want = lax.broadcasted_iota(jnp.int32, (size, tok), 0) + (start + j * half)
            pick = jnp.where(want == slot_ref[...], 1.0, 0.0).astype(BF16)
            send_ref[j, pl.ds(start, size), :] = mm(pick, rows_ref[...]).astype(BF16)


def combine(slot_row, back_ref):
    size = slot_row.shape[1]
    half = back_ref.shape[1]
    lane = lax.broadcasted_iota(jnp.int32, (size, 2 * half), 1)
    pick = jnp.where(lane == column(slot_row), 1.0, 0.0).astype(BF16)
    return mm(pick, back_ref[...].reshape(2 * half, back_ref.shape[2]))


ORDER = list(range(1, 64))


def step_kernel(cfg, *refs):
    n_pp, n_ep, side, tok, n_exp, cap, blk, chunk, eblk = cfg
    refs = list(refs)

    def take(n):
        got, refs[:] = refs[:n], refs[n:]
        return got

    ids_f, gate_f, ids_b, gate_b = take(4)
    hbm_in = take(8)
    y_out, dx_out, dwin_out, dwout_out, dwg_out, dwu_out, dwd_out = take(7)
    vm_in = take(8)
    grad, x_b, w_in, w_out, x_f, wg, wu, wd = vm_in
    in_sem, = take(1)
    slot_f, slot_b, rows_a, rows_b, h_f, h_b, y, dx = take(8)
    send_d, send_z, send_f, recv_d, recv_z, recv_f = take(6)
    send_dz, send_of, back_dz, back_of = take(4)
    dwg, dwu, dwd, acc_d = take(4)
    part, total, r1, r2, r3, turned = take(6)
    send_sem, recv_sem, local_sem, ar_send, ar_recv, pp_send, pp_recv, out_sem = take(8)

    me = lax.axis_index('ep')
    stage = lax.axis_index('pp')
    coord = [lax.rem(me, side), lax.rem(me // side, side), me // (side * side)]
    weight = [1, side, side * side]

    loads = [pltpu.make_async_copy(a, b, in_sem.at[i]) for i, (a, b) in enumerate(zip(hbm_in, vm_in))]
    for c in loads:
        c.start()

    barrier = pltpu.get_barrier_semaphore()

    @pl.loop(1, n_ep)
    def _(k):
        pl.semaphore_signal(barrier, inc=1, device_id={'ep': lax.rem(me + k, n_ep)}, device_id_type=MESH)

    nxt = lax.rem(stage + 1, n_pp)
    prv = lax.rem(stage + n_pp - 1, n_pp)
    pl.semaphore_signal(barrier, inc=1, device_id={'pp': nxt}, device_id_type=MESH)
    pl.semaphore_signal(barrier, inc=1, device_id={'pp': prv}, device_id_type=MESH)

    def rows_of(dev):
        return pl.ds(pl.multiple_of(dev * cap, cap), cap)

    def peer(k):
        to = 0
        for a in range(3):
            d = k // weight[a] % side
            to = to + weight[a] * lax.rem(coord[a] + lax.rem(stage * (side - d) + (1 - stage) * d, side), side)
        return to

    def start_exchange(x, src, dst):
        pltpu.make_async_copy(src.at[:, rows_of(me)], dst.at[:, rows_of(me)], local_sem.at[x]).start()
        for k in ORDER[:n_ep - 1] if n_ep == 64 else range(1, n_ep):
            to = peer(k)
            pltpu.make_async_remote_copy(
                src.at[:, rows_of(to)], dst.at[:, rows_of(me)], send_sem.at[x], recv_sem.at[x],
                device_id={'ep': to}, device_id_type=MESH).start()

    def most(ref):
        return ref.at[:, pl.ds(0, (n_ep - 1) * cap)]

    def wait_exchange(x, src, dst):
        pltpu.make_async_copy(src.at[:, rows_of(me)], dst.at[:, rows_of(me)], local_sem.at[x]).wait()
        pltpu.make_async_copy(most(dst), most(dst), recv_sem.at[x]).wait()

    def drain_exchange(x, src):
        pltpu.make_async_copy(most(src), most(src), send_sem.at[x]).wait()

    plan(ids_b, slot_b, n_exp, cap, blk)
    loads[0].wait()

    @pl.loop(0, tok // blk)
    def _(i):
        t = pl.ds(pl.multiple_of(i * blk, blk), blk)
        rows_a[t, :] = (column(gate_b[:, t]) * grad[t, :].astype(F32)).astype(BF16)

    dispatch(slot_b, rows_a, send_d, chunk)
    pl.semaphore_wait(barrier, n_ep + 1)
    start_exchange(0, send_d, recv_d)

    for c in loads[1:]:
        c.wait()

    def dense(x_ref, h_ref, z_ref):
        @pl.loop(0, tok // blk)
        def _(i):
            t = pl.ds(pl.multiple_of(i * blk, blk), blk)
            h = dense_tile(x_ref[t, :].astype(F32), w_in[...], w_out[...])
            h_ref[t, :] = h
            hf = h.astype(F32)
            z_ref[t, :] = (hf * inv_rms(hf)).astype(BF16)

    dense(x_b, h_b, rows_b)
    dispatch(slot_b, rows_b, send_z, chunk)
    start_exchange(1, send_z, recv_z)

    plan(ids_f, slot_f, n_exp, cap, blk)
    dense(x_f, h_f, rows_a)
    dispatch(slot_f, rows_a, send_f, chunk)
    start_exchange(2, send_f, recv_f)

    wait_exchange(0, send_d, recv_d)
    wait_exchange(1, send_z, recv_z)
    for e in range(2):
        dwg[e] = jnp.zeros(dwg.shape[1:], F32)
        dwu[e] = jnp.zeros(dwu.shape[1:], F32)
        acc_d[...] = jnp.zeros(acc_d.shape, F32)

        @pl.loop(0, n_ep * cap // eblk)
        def _(i):
            r = pl.ds(pl.multiple_of(i * eblk, eblk), eblk)
            x = recv_z[e, r, :]
            dy = recv_d[e, r, :]
            p = mm(x, wg[e])
            q = mm(x, wu[e])
            a = mm_nt(dy, wd[e])
            sig = jax.nn.sigmoid(p)
            act_g = p * sig
            act = (act_g * q).astype(BF16)
            dp = (a * q * (sig * (1.0 + p * (1.0 - sig)))).astype(BF16)
            dq = (a * act_g).astype(BF16)
            send_dz[e, r, :] = (mm_nt(dp, wg[e]) + mm_nt(dq, wu[e])).astype(BF16)
            dwg[e] += mm_tn(x, dp)
            dwu[e] += mm_tn(x, dq)
            acc_d[...] += mm_tn(dy, act)

        dwd[e] = jnp.transpose(acc_d[...])
    start_exchange(3, send_dz, back_dz)
    early = [pltpu.make_async_copy(a, b, out_sem.at[i]) for i, (a, b) in enumerate(((dwg, dwg_out), (dwu, dwu_out), (dwd, dwd_out)))]
    for c in early:
        c.start()

    wait_exchange(2, send_f, recv_f)
    for e in range(2):
        @pl.loop(0, n_ep * cap // eblk)
        def _(i):
            r = pl.ds(pl.multiple_of(i * eblk, eblk), eblk)
            x = recv_f[e, r, :]
            p = mm(x, wg[e])
            q = mm(x, wu[e])
            act = (p * jax.nn.sigmoid(p) * q).astype(BF16)
            send_of[e, r, :] = mm(act, wd[e]).astype(BF16)
    start_exchange(4, send_of, back_of)

    wait_exchange(3, send_dz, back_dz)
    hid = x_b.shape[1]
    cols = part.shape[2]
    part[...] = jnp.zeros(part.shape, F32)

    @pl.loop(0, tok // blk)
    def _(i):
        t = pl.ds(pl.multiple_of(i * blk, blk), blk)
        gz = combine(slot_b[:, t], back_dz)
        h = h_b[t, :].astype(F32)
        dh = grad[t, :].astype(F32) + rms_vjp(h, inv_rms(h), gz)
        b = dh.astype(BF16)
        x = x_b[t, :].astype(F32)
        inv = inv_rms(x)
        normed = (x * inv).astype(BF16)
        pre = mm(normed, w_in[...])
        sig = jax.nn.sigmoid(pre)
        act = (pre * sig).astype(BF16)
        da = (mm_nt(b, w_out[...]) * (sig * (1.0 + pre * (1.0 - sig)))).astype(BF16)
        dwin = mm_tn(normed, da)
        dwout = mm_tn(b, act)
        for q in range(3):
            part[q, :hid, :] += dwin[:, q * cols:(q + 1) * cols]
            part[q, hid:, :] += dwout[:, q * cols:(q + 1) * cols]
        dx[t, :] = (dh + rms_vjp(x, inv, mm_nt(da, w_in[...]))).astype(BF16)

    def to_stage(ref, out, i, s):
        return pltpu.make_async_remote_copy(ref, out, pp_send.at[i], pp_recv.at[i], device_id={'pp': s}, device_id_type=MESH)

    send_dx = to_stage(dx, dx_out, 0, prv)
    send_dx.start()

    rows = 2 * hid
    size = [rows // side, rows // side ** 2, rows // side ** 3]
    bufs = [r1, r2, r3]

    def base(q, depth):
        at = 0
        for j in range(depth):
            at = at + coord[(q + j) % 3] * size[j]
        return at

    def span(start, n):
        return pl.ds(pl.multiple_of(start, 8), n)

    def along(axis, d):
        c = lax.rem(coord[axis] + d, side)
        return c, me + (c - coord[axis]) * weight[axis]

    def scatter(q, j):
        axis = (q + j) % 3
        for d in range(1, side):
            c, to = along(axis, d)
            pltpu.make_async_remote_copy(
                part.at[q, span(base(q, j) + c * size[j], size[j])], bufs[j].at[q, d - 1],
                ar_send.at[j, q], ar_recv.at[j, q], device_id={'ep': to}, device_id_type=MESH).start()

    def scatter_wait(q, j):
        pltpu.make_async_copy(bufs[j].at[q], bufs[j].at[q], ar_recv.at[j, q]).wait()

    def add(q, j):
        s = span(base(q, j + 1), size[j])
        v = part[q, s, :]
        for d in range(side - 1):
            v = v + bufs[j][q, d]
        if j < 2:
            part[q, s, :] = v
        else:
            total[q, s, :] = v

    def gather(q, j):
        axis = (q + j) % 3
        s = span(base(q, j + 1), size[j])
        for d in range(1, side):
            c, to = along(axis, d)
            pltpu.make_async_remote_copy(
                total.at[q, s], total.at[q, s], ar_send.at[3 + j, q], ar_recv.at[3 + j, q],
                device_id={'ep': to}, device_id_type=MESH).start()

    def gather_wait(q, j):
        n = (side - 1) * size[j]
        pltpu.make_async_copy(total.at[q, pl.ds(0, n)], total.at[q, pl.ds(0, n)], ar_recv.at[3 + j, q]).wait()

    for q in range(3):
        scatter(q, 0)
    for j in range(3):
        for q in range(3):
            scatter_wait(q, j)
            add(q, j)
            if j < 2:
                scatter(q, j + 1)
            else:
                gather(q, 2)
    for j in (2, 1):
        for q in range(3):
            gather_wait(q, j)
            gather(q, j - 1)

    wait_exchange(4, send_of, back_of)

    @pl.loop(0, tok // blk)
    def _(i):
        t = pl.ds(pl.multiple_of(i * blk, blk), blk)
        picked = combine(slot_f[:, t], back_of)
        y[t, :] = (h_f[t, :].astype(F32) + picked * column(gate_f[:, t])).astype(BF16)

    send_y = to_stage(y, y_out, 1, nxt)
    send_y.start()

    late = []
    for q in range(3):
        gather_wait(q, 0)
        late.append(pltpu.make_async_copy(total.at[q, pl.ds(0, hid)], dwin_out.at[:, pl.ds(q * cols, cols)], out_sem.at[3 + q]))
        late[-1].start()
        turned[q * cols:(q + 1) * cols, :] = jnp.transpose(total[q, hid:, :])
    late.append(pltpu.make_async_copy(turned, dwout_out, out_sem.at[6]))
    late[-1].start()

    for x, src in enumerate((send_d, send_z, send_f, send_dz, send_of)):
        drain_exchange(x, src)
    for j in range(3):
        for q in range(3):
            n = pl.ds(0, (side - 1) * size[j])
            pltpu.make_async_copy(total.at[q, n], total.at[q, n], ar_send.at[j, q]).wait()
            pltpu.make_async_copy(total.at[q, n], total.at[q, n], ar_send.at[3 + j, q]).wait()
    for c in early + late:
        c.wait()
    send_dx.wait()
    send_y.wait()


def solution(mesh):
    n_ep = mesh.shape['ep']
    n_pp = mesh.shape['pp']
    side = round(n_ep ** (1 / 3))
    tok_spec = P('pp', 'ep', None)
    dense_spec = P('pp', None, None)
    exp_spec = P('pp', 'ep', None, None)

    def body(x_fwd, ids_fwd, gates_fwd, x_saved, grad_out, ids_bwd, gates_bwd, w_in, w_out, w_gate, w_up, w_down):
        x_fwd, x_saved, grad_out = x_fwd[0], x_saved[0], grad_out[0]
        w_in, w_out, w_gate, w_up, w_down = w_in[0], w_out[0], w_gate[0], w_up[0], w_down[0]
        tok, hid = x_fwd.shape
        ff = w_in.shape[1]
        n_exp = w_gate.shape[0] * n_ep
        eff = w_gate.shape[2]
        cap = 2 * tok // n_exp
        blk = min(256, tok)
        chunk = min(512, n_ep * cap)
        eblk = min(256, n_ep * cap)
        cfg = (n_pp, n_ep, side, tok, n_exp, cap, blk, chunk, eblk)
        ids_f, ids_b = ids_fwd.reshape(1, tok), ids_bwd.reshape(1, tok)
        gate_f, gate_b = gates_fwd.reshape(1, tok).astype(F32), gates_bwd.reshape(1, tok).astype(F32)
        big = [grad_out, x_saved, w_in, w_out, x_fwd, w_gate, w_up, w_down]
        slots = pltpu.VMEM((2, n_ep * cap, hid), BF16)
        rows = pltpu.VMEM((tok, hid), BF16)
        route = pltpu.VMEM((1, tok), jnp.int32)
        dma = pltpu.SemaphoreType.DMA
        cols = ff // 3
        outs = [((tok, hid), BF16)] * 2 + [(w.shape, F32) for w in (w_in, w_out, w_gate, w_up, w_down)]
        y_next, dx_prev, dw_in, dw_out, dw_gate, dw_up, dw_down = pl.pallas_call(
            functools.partial(step_kernel, cfg),
            out_shape=[jax.ShapeDtypeStruct(*o) for o in outs],
            in_specs=[VMEM] * 4 + [ANY] * 8,
            out_specs=[ANY] * 7,
            scratch_shapes=[pltpu.VMEM(b.shape, b.dtype) for b in big] + [dma((8,))]
            + [route] * 2 + [rows] * 6 + [slots] * 10
            + [pltpu.VMEM(w.shape, F32) for w in (w_gate, w_up, w_down)] + [pltpu.VMEM((hid, eff), F32)]
            + [pltpu.VMEM((3, 2 * hid, cols), F32)] * 2
            + [pltpu.VMEM((3, side - 1, 2 * hid // side ** j, cols), F32) for j in (1, 2, 3)]
            + [pltpu.VMEM((ff, hid), F32)]
            + [dma((5,)), dma((5,)), dma((5,)), dma((6, 3)), dma((6, 3)), dma((2,)), dma((2,)), dma((7,))],
            compiler_params=pltpu.CompilerParams(collective_id=0, has_side_effects=True, vmem_limit_bytes=63 * MIB),
        )(ids_f, gate_f, ids_b, gate_b, *big)
        return (y_next[None], dx_prev[None], dw_in[None], dw_out[None], dw_gate[None], dw_up[None], dw_down[None])

    return jax.shard_map(body, mesh=mesh,
                         in_specs=(tok_spec, tok_spec, tok_spec, tok_spec, tok_spec, tok_spec, tok_spec, dense_spec, dense_spec, exp_spec, exp_spec, exp_spec),
                         out_specs=(tok_spec, tok_spec, dense_spec, dense_spec, exp_spec, exp_spec, exp_spec),
                         check_vma=False)
```

time: 565 us -> 214 us (0.38); the launches traced: 555 us -> 213 us
  local copies, waits for them, and re-layouts: 222 us -> 11.1 us
  Pallas kernels: 0 us -> 201 us
  waiting for transfers between devices: 126 us -> 0 us
  other arithmetic: 84.7 us -> 0.62 us
  matrix products: 55.6 us -> 0 us
  starting transfers between devices: 50.8 us -> 0 us
  between operations: 15.4 us -> 0.67 us
    pallas_call x0 -> x1, Pallas kernels: none -> 201 us  [body(): pl.pallas_call(functools.partial(step_kernel, cfg), out_shape=[jax.ShapeD...]
    gather x16 -> x0, local copies, waits for them, and re-layouts: 170 us -> none  [the longest x3 50.4 us: gather_rows(): picked = jnp.take(tok_rows, src_tok, axis=0)]
    psum x1 -> x0, waiting for transfers between devices: 113 us -> none  [body(): dw_in = lax.psum(dw_in, 'ep')]
    dot_general x17 -> x0, matrix products: 55.6 us -> none  [the longest x1 7.85 us: expert_backward(): jnp.einsum('emf,emd->efd', act_bf, grad_rows, preferred_element_type=jnp....]
    all_to_all x5 -> x0, starting transfers between devices: 50 us -> none  [the longest x1 12.4 us: body(): lax.all_to_all(gather_rows(z_fwd, tok_f, valid_f), 'ep', 0, 1, tiled=True)]
    scatter-add x2 -> x0, other arithmetic: 30 us -> none  [route_plan(): counts = jnp.bincount(flat_ids, length=num_exp)]
    convert_element_type x4 -> x0, local copies, waits for them, and re-layouts: 22.1 us -> none  [the longest x1 14.2 us: expert_backward(): return (grad_in.astype(jnp.bfloat16), dw_gate, dw_up, dw_down)]
    sort x4 -> x0, other arithmetic: 20.9 us -> none  [the longest x2 10.8 us: route_plan(): route_order = jnp.argsort(flat_ids, stable=True)]
  transfers between devices with their start and end apart: 8 -> 0, of which waited for: 4 -> 0; matrix products, arithmetic and copies ran while one was open for 43% -> 0% of each run, Pallas kernels for 0% -> 0%
where the time goes in v3:
time: 214 us; the launch traced here: 213 us
  Pallas kernels  201 us (94%)
  local copies, waits for them, and re-layouts  11.1 us (5%)
    pallas_call x1, Pallas kernels, body(): pl.pallas_call(functools.partial(step_kernel, cfg), out_shape=[jax.ShapeD...  201 us
    unnamed x23, local copies, waits for them, and re-layouts  11.1 us

profile of v3, /device:TPU:1, one launch (start us, length us, event | category | flops | bytes accessed | tf_op | source)
XLA Modules:
  0.0 213.3 jit_solution(8345147585228863249)
XLA Ops:
  0.6 0.0 copy-start.7
  0.6 0.0 copy-start.6
  0.7 0.7 copy-done.7
  1.3 0.0 copy-done.6
  1.3 0.6 bitcast_convert_fusion
  2.0 200.9 %shard_map.171 = (bf16[2048,256]{1,0:T(8,128)(2,1)}, bf16[2048,256]{1,0:T(8,128)(2,1)}, f32[256,768]{1,0:T(8,128)}, f32[768,256]{1,0:T(8,128)}, f32[2,256,384]{2...) custom-call(s32[1,2048]{1,0:T(1,128)} %bitcast.38, f32[1,2048]{1,0:T(1,128)} %get-tuple-element.22.refs_1_, ...), custom_call_target="tpu_custom_call" | custom-call | tf_op jit(solution)/shard_map/pallas_call | solution.py:396
  202.9 0.0 copy-start
  202.9 2.4 %copy.26 = bf16[1,2048,256]{2,1,0:T(8,128)(2,1)} copy(bf16[1,2048,256]{2,1,0:T(8,128)(2,1)} %bitcast.27) | data formatting | bytes 2097152
  205.3 0.0 copy-done
  205.3 0.0 copy-start.5
  205.3 1.0 copy.27
  206.2 0.5 copy-done.5
  206.8 0.0 copy-start.4
  206.8 0.9 copy.28
  207.7 0.5 copy-done.4
  208.2 0.0 copy-start.3
  208.2 0.9 copy.29
  209.1 0.5 copy-done.3
  209.6 0.0 copy-start.2
  209.6 0.9 copy.30
  210.5 0.5 copy-done.2
  211.0 0.0 copy-start.1
  211.0 0.9 copy.31
  211.9 0.5 copy-done.1
  212.4 0.9 copy.32
Async XLA Ops:
  0.6 0.7 copy-start.7
  0.6 0.7 copy-start.6
  202.9 2.4 %copy-start = (bf16[2048,256]{1,0:T(8,128)(2,1)S(1)}, bf16[2048,256]{1,0:T(8,128)(2,1)}, u32[]{:S(2)}) copy-start(bf16[2048,256]{1,0:T(8,128)(2,1)} %get-tuple-element.15) | copy-start | bytes 3145732
  205.3 1.5 copy-start.5
  206.8 1.4 copy-start.4
  208.2 1.4 copy-start.3
  209.6 1.4 copy-start.2
  211.0 1.4 copy-start.1

commit v4 on v3

--- a/solution.py
+++ b/solution.py
@@ -65,27 +65,31 @@
     return h
 
 
-def dispatch(slot_ref, rows_ref, send_ref, size):
+def dispatch(slot_ref, rows_ref, send_ref, j, size):
     tok = slot_ref.shape[1]
     half = send_ref.shape[1]
-    for j in range(2):
-        @pl.loop(0, half // size)
-        def _(c):
-            start = pl.multiple_of(c * size, size)
-            want = lax.broadcasted_iota(jnp.int32, (size, tok), 0) + (start + j * half)
-            pick = jnp.where(want == slot_ref[...], 1.0, 0.0).astype(BF16)
-            send_ref[j, pl.ds(start, size), :] = mm(pick, rows_ref[...]).astype(BF16)
-
-
-def combine(slot_row, back_ref):
+
+    @pl.loop(0, half // size)
+    def _(c):
+        start = pl.multiple_of(c * size, size)
+        want = lax.broadcasted_iota(jnp.int32, (size, tok), 0) + (start + j * half)
+        pick = jnp.where(want == slot_ref[...], 1.0, 0.0).astype(BF16)
+        send_ref[j, pl.ds(start, size), :] = mm(pick, rows_ref[...]).astype(BF16)
+
+
+def combine(slot_row, back_ref, j):
     size = slot_row.shape[1]
     half = back_ref.shape[1]
-    lane = lax.broadcasted_iota(jnp.int32, (size, 2 * half), 1)
+    lane = lax.broadcasted_iota(jnp.int32, (size, half), 1) + j * half
     pick = jnp.where(lane == column(slot_row), 1.0, 0.0).astype(BF16)
-    return mm(pick, back_ref[...].reshape(2 * half, back_ref.shape[2]))
-
-
-ORDER = list(range(1, 64))
+    return mm(pick, back_ref[j])
+
+
+ORDER = (
+    14, 16, 44, 28, 25, 36, 1, 51, 10, 6, 50, 2, 9, 24, 32, 39, 18, 49, 33, 37, 48,
+    12, 60, 41, 40, 8, 61, 13, 29, 62, 22, 59, 7, 20, 21, 63, 31, 45, 5, 26, 34, 47,
+    46, 54, 17, 52, 58, 3, 56, 57, 35, 38, 4, 53, 55, 27, 23, 19, 11, 15, 30, 43, 42,
+)
 
 
 def step_kernel(cfg, *refs):
@@ -107,6 +111,7 @@
     send_dz, send_of, back_dz, back_of = take(4)
     dwg, dwu, dwd, acc_d = take(4)
     part, total, r1, r2, r3, turned = take(6)
+    normed_b, act_b, slope_b, gz_b, gz_f = take(5)
     send_sem, recv_sem, local_sem, ar_send, ar_recv, pp_send, pp_recv, out_sem = take(8)
 
     me = lax.axis_index('ep')
@@ -139,23 +144,30 @@
             to = to + weight[a] * lax.rem(coord[a] + lax.rem(stage * (side - d) + (1 - stage) * d, side), side)
         return to
 
-    def start_exchange(x, src, dst):
-        pltpu.make_async_copy(src.at[:, rows_of(me)], dst.at[:, rows_of(me)], local_sem.at[x]).start()
-        for k in ORDER[:n_ep - 1] if n_ep == 64 else range(1, n_ep):
+    order = ORDER if n_ep == 64 else range(1, n_ep)
+
+    def own(x, j, src, dst):
+        return pltpu.make_async_copy(src.at[j, rows_of(me)], dst.at[j, rows_of(me)], local_sem.at[x, j])
+
+    def start_exchange(x, j, src, dst, piece=0, pieces=1):
+        if piece == 0:
+            own(x, j, src, dst).start()
+        n = len(order)
+        for k in order[n * piece // pieces:n * (piece + 1) // pieces]:
             to = peer(k)
             pltpu.make_async_remote_copy(
-                src.at[:, rows_of(to)], dst.at[:, rows_of(me)], send_sem.at[x], recv_sem.at[x],
+                src.at[j, rows_of(to)], dst.at[j, rows_of(me)], send_sem.at[x, j], recv_sem.at[x, j],
                 device_id={'ep': to}, device_id_type=MESH).start()
 
-    def most(ref):
-        return ref.at[:, pl.ds(0, (n_ep - 1) * cap)]
-
-    def wait_exchange(x, src, dst):
-        pltpu.make_async_copy(src.at[:, rows_of(me)], dst.at[:, rows_of(me)], local_sem.at[x]).wait()
-        pltpu.make_async_copy(most(dst), most(dst), recv_sem.at[x]).wait()
-
-    def drain_exchange(x, src):
-        pltpu.make_async_copy(most(src), most(src), send_sem.at[x]).wait()
+    def most(ref, j):
+        return ref.at[j, pl.ds(0, (n_ep - 1) * cap)]
+
+    def wait_exchange(x, j, src, dst):
+        own(x, j, src, dst).wait()
+        pltpu.make_async_copy(most(dst, j), most(dst, j), recv_sem.at[x, j]).wait()
+
+    def drain_exchange(x, j, src):
+        pltpu.make_async_copy(most(src, j), most(src, j), send_sem.at[x, j]).wait()
 
     plan(ids_b, slot_b, n_exp, cap, blk)
     loads[0].wait()
@@ -163,36 +175,52 @@
     @pl.loop(0, tok // blk)
     def _(i):
         t = pl.ds(pl.multiple_of(i * blk, blk), blk)
-        rows_a[t, :] = (column(gate_b[:, t]) * grad[t, :].astype(F32)).astype(BF16)
-
-    dispatch(slot_b, rows_a, send_d, chunk)
+        rows_a[t, :] = (column(gate_b[:, t].astype(F32)) * grad[t, :].astype(F32)).astype(BF16)
+
+    dispatch(slot_b, rows_a, send_d, 0, chunk)
     pl.semaphore_wait(barrier, n_ep + 1)
-    start_exchange(0, send_d, recv_d)
+    start_exchange(0, 0, send_d, recv_d)
 
     for c in loads[1:]:
         c.wait()
 
-    def dense(x_ref, h_ref, z_ref):
-        @pl.loop(0, tok // blk)
-        def _(i):
-            t = pl.ds(pl.multiple_of(i * blk, blk), blk)
-            h = dense_tile(x_ref[t, :].astype(F32), w_in[...], w_out[...])
-            h_ref[t, :] = h
-            hf = h.astype(F32)
-            z_ref[t, :] = (hf * inv_rms(hf)).astype(BF16)
-
-    dense(x_b, h_b, rows_b)
-    dispatch(slot_b, rows_b, send_z, chunk)
-    start_exchange(1, send_z, recv_z)
+    @pl.loop(0, tok // blk)
+    def _(i):
+        t = pl.ds(pl.multiple_of(i * blk, blk), blk)
+        x = x_b[t, :].astype(F32)
+        normed = (x * inv_rms(x)).astype(BF16)
+        pre = mm(normed, w_in[...])
+        sig = jax.nn.sigmoid(pre)
+        act = (pre * sig).astype(BF16)
+        normed_b[t, :] = normed
+        act_b[t, :] = act
+        slope_b[t, :] = sig * (1.0 + pre * (1.0 - sig))
+        h = (x + mm(act, w_out[...])).astype(BF16)
+        h_b[t, :] = h
+        hf = h.astype(F32)
+        rows_b[t, :] = (hf * inv_rms(hf)).astype(BF16)
+
+    dispatch(slot_b, rows_b, send_z, 0, chunk)
+    start_exchange(1, 0, send_z, recv_z)
+    dispatch(slot_b, rows_a, send_d, 1, chunk)
+    start_exchange(0, 1, send_d, recv_d)
+    dispatch(slot_b, rows_b, send_z, 1, chunk)
+    start_exchange(1, 1, send_z, recv_z)
 
     plan(ids_f, slot_f, n_exp, cap, blk)
-    dense(x_f, h_f, rows_a)
-    dispatch(slot_f, rows_a, send_f, chunk)
-    start_exchange(2, send_f, recv_f)
-
-    wait_exchange(0, send_d, recv_d)
-    wait_exchange(1, send_z, recv_z)
-    for e in range(2):
+
+    @pl.loop(0, tok // blk)
+    def _(i):
+        t = pl.ds(pl.multiple_of(i * blk, blk), blk)
+        h = dense_tile(x_f[t, :].astype(F32), w_in[...], w_out[...])
+        h_f[t, :] = h
+        hf = h.astype(F32)
+        rows_a[t, :] = (hf * inv_rms(hf)).astype(BF16)
+
+    for j in range(2):
+        dispatch(slot_f, rows_a, send_f, j, chunk)
+
+    def expert_backward(e):
         dwg[e] = jnp.zeros(dwg.shape[1:], F32)
         dwu[e] = jnp.zeros(dwu.shape[1:], F32)
         acc_d[...] = jnp.zeros(acc_d.shape, F32)
@@ -216,13 +244,8 @@
             acc_d[...] += mm_tn(dy, act)
 
         dwd[e] = jnp.transpose(acc_d[...])
-    start_exchange(3, send_dz, back_dz)
-    early = [pltpu.make_async_copy(a, b, out_sem.at[i]) for i, (a, b) in enumerate(((dwg, dwg_out), (dwu, dwu_out), (dwd, dwd_out)))]
-    for c in early:
-        c.start()
-
-    wait_exchange(2, send_f, recv_f)
-    for e in range(2):
+
+    def expert_forward(e):
         @pl.loop(0, n_ep * cap // eblk)
         def _(i):
             r = pl.ds(pl.multiple_of(i * eblk, eblk), eblk)
@@ -231,33 +254,47 @@
             q = mm(x, wu[e])
             act = (p * jax.nn.sigmoid(p) * q).astype(BF16)
             send_of[e, r, :] = mm(act, wd[e]).astype(BF16)
-    start_exchange(4, send_of, back_of)
-
-    wait_exchange(3, send_dz, back_dz)
+
+    for e in range(2):
+        wait_exchange(0, e, send_d, recv_d)
+        wait_exchange(1, e, send_z, recv_z)
+        expert_backward(e)
+        start_exchange(3, e, send_dz, back_dz)
+    start_exchange(2, 0, send_f, recv_f)
+    early = [pltpu.make_async_copy(a, b, out_sem.at[i]) for i, (a, b) in enumerate(((dwg, dwg_out), (dwu, dwu_out), (dwd, dwd_out)))]
+    for c in early:
+        c.start()
+
     hid = x_b.shape[1]
     cols = part.shape[2]
     part[...] = jnp.zeros(part.shape, F32)
 
+    def combine_half(x, j, src, back, slot, acc):
+        wait_exchange(x, j, src, back)
+
+        @pl.loop(0, tok // blk)
+        def _(i):
+            t = pl.ds(pl.multiple_of(i * blk, blk), blk)
+            acc[t, :] = combine(slot[:, t], back, j)
+
+    combine_half(3, 0, send_dz, back_dz, slot_b, gz_b)
+    wait_exchange(3, 1, send_dz, back_dz)
+
     @pl.loop(0, tok // blk)
     def _(i):
         t = pl.ds(pl.multiple_of(i * blk, blk), blk)
-        gz = combine(slot_b[:, t], back_dz)
+        gz = gz_b[t, :] + combine(slot_b[:, t], back_dz, 1)
         h = h_b[t, :].astype(F32)
         dh = grad[t, :].astype(F32) + rms_vjp(h, inv_rms(h), gz)
         b = dh.astype(BF16)
-        x = x_b[t, :].astype(F32)
-        inv = inv_rms(x)
-        normed = (x * inv).astype(BF16)
-        pre = mm(normed, w_in[...])
-        sig = jax.nn.sigmoid(pre)
-        act = (pre * sig).astype(BF16)
-        da = (mm_nt(b, w_out[...]) * (sig * (1.0 + pre * (1.0 - sig)))).astype(BF16)
-        dwin = mm_tn(normed, da)
-        dwout = mm_tn(b, act)
+        da = (mm_nt(b, w_out[...]) * slope_b[t, :]).astype(BF16)
+        dwin = mm_tn(normed_b[t, :], da)
+        dwout = mm_tn(b, act_b[t, :])
         for q in range(3):
             part[q, :hid, :] += dwin[:, q * cols:(q + 1) * cols]
             part[q, hid:, :] += dwout[:, q * cols:(q + 1) * cols]
-        dx[t, :] = (dh + rms_vjp(x, inv, mm_nt(da, w_in[...]))).astype(BF16)
+        x = x_b[t, :].astype(F32)
+        dx[t, :] = (dh + rms_vjp(x, inv_rms(x), mm_nt(da, w_in[...]))).astype(BF16)
 
     def to_stage(ref, out, i, s):
         return pltpu.make_async_remote_copy(ref, out, pp_send.at[i], pp_recv.at[i], device_id={'pp': s}, device_id_type=MESH)
@@ -318,6 +355,8 @@
 
     for q in range(3):
         scatter(q, 0)
+    start_exchange(2, 1, send_f, recv_f, 0, 3)
+    wait_exchange(2, 0, send_f, recv_f)
     for j in range(3):
         for q in range(3):
             scatter_wait(q, j)
@@ -326,22 +365,20 @@
                 scatter(q, j + 1)
             else:
                 gather(q, 2)
+        if j < 2:
+            start_exchange(2, 1, send_f, recv_f, j + 1, 3)
+        if j == 0:
+            expert_forward(0)
+    start_exchange(4, 0, send_of, back_of, 0, 3)
     for j in (2, 1):
         for q in range(3):
             gather_wait(q, j)
             gather(q, j - 1)
-
-    wait_exchange(4, send_of, back_of)
-
-    @pl.loop(0, tok // blk)
-    def _(i):
-        t = pl.ds(pl.multiple_of(i * blk, blk), blk)
-        picked = combine(slot_f[:, t], back_of)
-        y[t, :] = (h_f[t, :].astype(F32) + picked * column(gate_f[:, t])).astype(BF16)
-
-    send_y = to_stage(y, y_out, 1, nxt)
-    send_y.start()
-
+        start_exchange(4, 0, send_of, back_of, 3 - j, 3)
+
+    wait_exchange(2, 1, send_f, recv_f)
+    expert_forward(1)
+    start_exchange(4, 1, send_of, back_of)
     late = []
     for q in range(3):
         gather_wait(q, 0)
@@ -351,8 +388,21 @@
     late.append(pltpu.make_async_copy(turned, dwout_out, out_sem.at[6]))
     late[-1].start()
 
+    combine_half(4, 0, send_of, back_of, slot_f, gz_f)
+    wait_exchange(4, 1, send_of, back_of)
+
+    @pl.loop(0, tok // blk)
+    def _(i):
+        t = pl.ds(pl.multiple_of(i * blk, blk), blk)
+        picked = gz_f[t, :] + combine(slot_f[:, t], back_of, 1)
+        y[t, :] = (h_f[t, :].astype(F32) + picked * column(gate_f[:, t].astype(F32))).astype(BF16)
+
+    send_y = to_stage(y, y_out, 1, nxt)
+    send_y.start()
+
     for x, src in enumerate((send_d, send_z, send_f, send_dz, send_of)):
-        drain_exchange(x, src)
+        for j in range(2):
+            drain_exchange(x, j, src)
     for j in range(3):
         for q in range(3):
             n = pl.ds(0, (side - 1) * size[j])
@@ -362,6 +412,29 @@
         c.wait()
     send_dx.wait()
     send_y.wait()
+
+
+def write_kernel(n, *refs):
+    ins, outs, hold, sem = refs[:n], refs[n:2 * n], refs[2 * n:3 * n], refs[3 * n]
+    gets = [pltpu.make_async_copy(ins[i], hold[i], sem.at[0, i]) for i in range(n)]
+    puts = [pltpu.make_async_copy(hold[i], outs[i], sem.at[1, i]) for i in range(n)]
+    for c in gets:
+        c.start()
+    for get, put in zip(gets, puts):
+        get.wait()
+        put.start()
+    for c in puts:
+        c.wait()
+
+
+def write(*arrays):
+    n = len(arrays)
+    shapes = [jax.ShapeDtypeStruct(a.shape, a.dtype) for a in arrays]
+    return pl.pallas_call(
+        functools.partial(write_kernel, n), out_shape=shapes, in_specs=[ANY] * n, out_specs=[ANY] * n,
+        scratch_shapes=[pltpu.VMEM(a.shape, a.dtype) for a in arrays] + [pltpu.SemaphoreType.DMA((2, n))],
+        compiler_params=pltpu.CompilerParams(vmem_limit_bytes=62 * MIB),
+    )(*arrays)
 
 
 def solution(mesh):
@@ -382,10 +455,10 @@
         cap = 2 * tok // n_exp
         blk = min(256, tok)
         chunk = min(512, n_ep * cap)
-        eblk = min(256, n_ep * cap)
+        eblk = min(512, n_ep * cap)
         cfg = (n_pp, n_ep, side, tok, n_exp, cap, blk, chunk, eblk)
         ids_f, ids_b = ids_fwd.reshape(1, tok), ids_bwd.reshape(1, tok)
-        gate_f, gate_b = gates_fwd.reshape(1, tok).astype(F32), gates_bwd.reshape(1, tok).astype(F32)
+        gate_f, gate_b = gates_fwd.reshape(1, tok), gates_bwd.reshape(1, tok)
         big = [grad_out, x_saved, w_in, w_out, x_fwd, w_gate, w_up, w_down]
         slots = pltpu.VMEM((2, n_ep * cap, hid), BF16)
         rows = pltpu.VMEM((tok, hid), BF16)
@@ -393,7 +466,7 @@
         dma = pltpu.SemaphoreType.DMA
         cols = ff // 3
         outs = [((tok, hid), BF16)] * 2 + [(w.shape, F32) for w in (w_in, w_out, w_gate, w_up, w_down)]
-        y_next, dx_prev, dw_in, dw_out, dw_gate, dw_up, dw_down = pl.pallas_call(
+        results = pl.pallas_call(
             functools.partial(step_kernel, cfg),
             out_shape=[jax.ShapeDtypeStruct(*o) for o in outs],
             in_specs=[VMEM] * 4 + [ANY] * 8,
@@ -404,9 +477,11 @@
             + [pltpu.VMEM((3, 2 * hid, cols), F32)] * 2
             + [pltpu.VMEM((3, side - 1, 2 * hid // side ** j, cols), F32) for j in (1, 2, 3)]
             + [pltpu.VMEM((ff, hid), F32)]
-            + [dma((5,)), dma((5,)), dma((5,)), dma((6, 3)), dma((6, 3)), dma((2,)), dma((2,)), dma((7,))],
+            + [rows, pltpu.VMEM((tok, ff), BF16), pltpu.VMEM((tok, ff), F32), pltpu.VMEM((tok, hid), F32), pltpu.VMEM((tok, hid), F32)]
+            + [dma((5, 2)), dma((5, 2)), dma((5, 2)), dma((6, 3)), dma((6, 3)), dma((2,)), dma((2,)), dma((7,))],
             compiler_params=pltpu.CompilerParams(collective_id=0, has_side_effects=True, vmem_limit_bytes=63 * MIB),
         )(ids_f, gate_f, ids_b, gate_b, *big)
+        y_next, dx_prev, dw_in, dw_out, dw_gate, dw_up, dw_down = write(*results)
         return (y_next[None], dx_prev[None], dw_in[None], dw_out[None], dw_gate[None], dw_up[None], dw_down[None])
 
     return jax.shard_map(body, mesh=mesh,

time: 214 us -> 189 us (0.88)
  Pallas kernels: 201 us -> 186 us
  local copies, waits for them, and re-layouts: 11.1 us -> 0 us
    pallas_call x1, Pallas kernels: 201 us -> 181 us  [body(): pl.pallas_call(functools.partial(step_kernel, cfg), out_shape=[jax.ShapeD...]
    unnamed x23 -> x0, local copies, waits for them, and re-layouts: 11.1 us -> none
    pallas_call x0 -> x1, Pallas kernels: none -> 5.11 us  [write(): pl.pallas_call(functools.partial(write_kernel, n), out_shape=shapes, in_s...]
where the time goes in v4:
time: 189 us; the launch traced here: 187 us
  Pallas kernels  186 us (98%)
    pallas_call x1, Pallas kernels, body(): pl.pallas_call(functools.partial(step_kernel, cfg), out_shape=[jax.ShapeD...  181 us
    pallas_call x1, Pallas kernels, write(): pl.pallas_call(functools.partial(write_kernel, n), out_shape=shapes, in_s...  5.11 us

profile of v4, /device:TPU:1, one launch (start us, length us, event | category | flops | bytes accessed | tf_op | source)
XLA Modules:
  0.0 186.6 jit_solution(6171597403604076918)
XLA Ops:
  0.6 180.7 %shard_map.171 = (bf16[2048,256]{1,0:T(8,128)(2,1)}, bf16[2048,256]{1,0:T(8,128)(2,1)}, f32[256,768]{1,0:T(8,128)}, f32[768,256]{1,0:T(8,128)}, f32[2,256,384]{2...) custom-call(s32[1,2048]{1,0:T(1,128)} %bitcast.27, bf16[1,2048]{1,0:T(2,128)(2,1)} %bitcast.28, ...), custom_call_target="tpu_custom_call" | custom-call | tf_op jit(solution)/shard_map/pallas_call | solution.py:469
  181.3 5.1 %shard_map.172 = (bf16[2048,256]{1,0:T(8,128)(2,1)}, bf16[2048,256]{1,0:T(8,128)(2,1)}, f32[256,768]{1,0:T(8,128)}, f32[768,256]{1,0:T(8,128)}, f32[2,256,384]{2...) custom-call(bf16[2048,256]{1,0:T(8,128)(2,1)} %get-tuple-element.21.refs_0_, ...), custom_call_target="tpu_custom_call" | custom-call | tf_op jit(solution)/shard_map/pallas_call | solution.py:433

commit v5 on v4

--- a/solution.py
+++ b/solution.py
@@ -260,7 +260,8 @@
         wait_exchange(1, e, send_z, recv_z)
         expert_backward(e)
         start_exchange(3, e, send_dz, back_dz)
-    start_exchange(2, 0, send_f, recv_f)
+    for e in range(2):
+        start_exchange(2, e, send_f, recv_f)
     early = [pltpu.make_async_copy(a, b, out_sem.at[i]) for i, (a, b) in enumerate(((dwg, dwg_out), (dwu, dwu_out), (dwd, dwd_out)))]
     for c in early:
         c.start()
@@ -355,8 +356,11 @@
 
     for q in range(3):
         scatter(q, 0)
-    start_exchange(2, 1, send_f, recv_f, 0, 3)
     wait_exchange(2, 0, send_f, recv_f)
+    expert_forward(0)
+    start_exchange(4, 0, send_of, back_of, 0, 2)
+    wait_exchange(2, 1, send_f, recv_f)
+    expert_forward(1)
     for j in range(3):
         for q in range(3):
             scatter_wait(q, j)
@@ -365,20 +369,24 @@
                 scatter(q, j + 1)
             else:
                 gather(q, 2)
-        if j < 2:
-            start_exchange(2, 1, send_f, recv_f, j + 1, 3)
-        if j == 0:
-            expert_forward(0)
-    start_exchange(4, 0, send_of, back_of, 0, 3)
+        start_exchange(4, (j + 1) // 2, send_of, back_of, (j + 1) % 2, 2)
     for j in (2, 1):
         for q in range(3):
             gather_wait(q, j)
             gather(q, j - 1)
-        start_exchange(4, 0, send_of, back_of, 3 - j, 3)
-
-    wait_exchange(2, 1, send_f, recv_f)
-    expert_forward(1)
-    start_exchange(4, 1, send_of, back_of)
+
+    combine_half(4, 0, send_of, back_of, slot_f, gz_f)
+    wait_exchange(4, 1, send_of, back_of)
+
+    @pl.loop(0, tok // blk)
+    def _(i):
+        t = pl.ds(pl.multiple_of(i * blk, blk), blk)
+        picked = gz_f[t, :] + combine(slot_f[:, t], back_of, 1)
+        y[t, :] = (h_f[t, :].astype(F32) + picked * column(gate_f[:, t].astype(F32))).astype(BF16)
+
+    send_y = to_stage(y, y_out, 1, nxt)
+    send_y.start()
+
     late = []
     for q in range(3):
         gather_wait(q, 0)
@@ -387,18 +395,6 @@
         turned[q * cols:(q + 1) * cols, :] = jnp.transpose(total[q, hid:, :])
     late.append(pltpu.make_async_copy(turned, dwout_out, out_sem.at[6]))
     late[-1].start()
-
-    combine_half(4, 0, send_of, back_of, slot_f, gz_f)
-    wait_exchange(4, 1, send_of, back_of)
-
-    @pl.loop(0, tok // blk)
-    def _(i):
-        t = pl.ds(pl.multiple_of(i * blk, blk), blk)
-        picked = gz_f[t, :] + combine(slot_f[:, t], back_of, 1)
-        y[t, :] = (h_f[t, :].astype(F32) + picked * column(gate_f[:, t].astype(F32))).astype(BF16)
-
-    send_y = to_stage(y, y_out, 1, nxt)
-    send_y.start()
 
     for x, src in enumerate((send_d, send_z, send_f, send_dz, send_of)):
         for j in range(2):

time: 189 us -> 176 us (0.931); the launches traced: 187 us -> 176 us
  Pallas kernels: 186 us -> 175 us
    pallas_call x1, Pallas kernels: 181 us -> 170 us  [body(): pl.pallas_call(functools.partial(step_kernel, cfg), out_shape=[jax.ShapeD...]
where the time goes in v5:
time: 176 us
  Pallas kernels  175 us (99%)
    pallas_call x1, Pallas kernels, body(): pl.pallas_call(functools.partial(step_kernel, cfg), out_shape=[jax.ShapeD...  170 us
    pallas_call x1, Pallas kernels, write(): pl.pallas_call(functools.partial(write_kernel, n), out_shape=shapes, in_s...  5.11 us

profile of v5, /device:TPU:1, one launch (start us, length us, event | category | flops | bytes accessed | tf_op | source)
XLA Modules:
  0.0 175.8 jit_solution(14625944206042779576)
XLA Ops:
  0.6 169.9 %shard_map.171 = (bf16[2048,256]{1,0:T(8,128)(2,1)}, bf16[2048,256]{1,0:T(8,128)(2,1)}, f32[256,768]{1,0:T(8,128)}, f32[768,256]{1,0:T(8,128)}, f32[2,256,384]{2...) custom-call(s32[1,2048]{1,0:T(1,128)} %bitcast.27, bf16[1,2048]{1,0:T(2,128)(2,1)} %bitcast.28, ...), custom_call_target="tpu_custom_call" | custom-call | tf_op jit(solution)/shard_map/pallas_call | solution.py:465
  170.5 5.1 %shard_map.172 = (bf16[2048,256]{1,0:T(8,128)(2,1)}, bf16[2048,256]{1,0:T(8,128)(2,1)}, f32[256,768]{1,0:T(8,128)}, f32[768,256]{1,0:T(8,128)}, f32[2,256,384]{2...) custom-call(bf16[2048,256]{1,0:T(8,128)(2,1)} %get-tuple-element.21.refs_0_, ...), custom_call_target="tpu_custom_call" | custom-call | tf_op jit(solution)/shard_map/pallas_call | solution.py:429

commit v6 on v5

--- a/solution.py
+++ b/solution.py
@@ -110,7 +110,7 @@
     send_d, send_z, send_f, recv_d, recv_z, recv_f = take(6)
     send_dz, send_of, back_dz, back_of = take(4)
     dwg, dwu, dwd, acc_d = take(4)
-    part, total, r1, r2, r3, turned = take(6)
+    part, total, r1, r2, turned = take(5)
     normed_b, act_b, slope_b, gz_b, gz_f = take(5)
     send_sem, recv_sem, local_sem, ar_send, ar_recv, pp_send, pp_recv, out_sem = take(8)
 
@@ -260,8 +260,8 @@
         wait_exchange(1, e, send_z, recv_z)
         expert_backward(e)
         start_exchange(3, e, send_dz, back_dz)
-    for e in range(2):
-        start_exchange(2, e, send_f, recv_f)
+    start_exchange(2, 0, send_f, recv_f)
+    start_exchange(2, 1, send_f, recv_f, 0, 2)
     early = [pltpu.make_async_copy(a, b, out_sem.at[i]) for i, (a, b) in enumerate(((dwg, dwg_out), (dwu, dwu_out), (dwd, dwd_out)))]
     for c in early:
         c.start()
@@ -304,76 +304,83 @@
     send_dx.start()
 
     rows = 2 * hid
-    size = [rows // side, rows // side ** 2, rows // side ** 3]
-    bufs = [r1, r2, r3]
-
-    def base(q, depth):
-        at = 0
-        for j in range(depth):
-            at = at + coord[(q + j) % 3] * size[j]
-        return at
+    wide, narrow = rows // side, rows // side ** 3
+    plane = [(b, c) for b in range(side) for c in range(side)][1:]
 
     def span(start, n):
         return pl.ds(pl.multiple_of(start, 8), n)
 
-    def along(axis, d):
-        c = lax.rem(coord[axis] + d, side)
-        return c, me + (c - coord[axis]) * weight[axis]
-
-    def scatter(q, j):
-        axis = (q + j) % 3
+    def row_of(q, b, c):
+        return coord[q] * wide + (b * side + c) * narrow
+
+    def shifted(axis, d):
+        return lax.rem(coord[axis] + d, side)
+
+    def push(src, dst, phase, q, to):
+        pltpu.make_async_remote_copy(src, dst, ar_send.at[phase, q], ar_recv.at[phase, q], device_id={'ep': to}, device_id_type=MESH).start()
+
+    def plane_peers(q):
+        b0, c0 = (q + 1) % 3, (q + 2) % 3
+        for i, (db, dc) in enumerate(plane):
+            b, c = shifted(b0, db), shifted(c0, dc)
+            yield i, b, c, me + (b - coord[b0]) * weight[b0] + (c - coord[c0]) * weight[c0]
+
+    def mine(q):
+        return span(row_of(q, coord[(q + 1) % 3], coord[(q + 2) % 3]), narrow)
+
+    def scatter_axis(q):
         for d in range(1, side):
-            c, to = along(axis, d)
-            pltpu.make_async_remote_copy(
-                part.at[q, span(base(q, j) + c * size[j], size[j])], bufs[j].at[q, d - 1],
-                ar_send.at[j, q], ar_recv.at[j, q], device_id={'ep': to}, device_id_type=MESH).start()
-
-    def scatter_wait(q, j):
-        pltpu.make_async_copy(bufs[j].at[q], bufs[j].at[q], ar_recv.at[j, q]).wait()
-
-    def add(q, j):
-        s = span(base(q, j + 1), size[j])
+            c = shifted(q, d)
+            push(part.at[q, span(c * wide, wide)], r1.at[q, d - 1], 0, q, me + (c - coord[q]) * weight[q])
+
+    def scatter_plane(q):
+        pltpu.make_async_copy(r1.at[q], r1.at[q], ar_recv.at[0, q]).wait()
+        s = span(coord[q] * wide, wide)
         v = part[q, s, :]
         for d in range(side - 1):
-            v = v + bufs[j][q, d]
-        if j < 2:
-            part[q, s, :] = v
-        else:
-            total[q, s, :] = v
-
-    def gather(q, j):
-        axis = (q + j) % 3
-        s = span(base(q, j + 1), size[j])
+            v = v + r1[q, d]
+        part[q, s, :] = v
+        for i, b, c, to in plane_peers(q):
+            push(part.at[q, span(row_of(q, b, c), narrow)], r2.at[q, i], 1, q, to)
+
+    def gather_plane(q):
+        pltpu.make_async_copy(r2.at[q], r2.at[q], ar_recv.at[1, q]).wait()
+        v = part[q, mine(q), :]
+        for i in range(len(plane)):
+            v = v + r2[q, i]
+        total[q, mine(q), :] = v
+        for i, b, c, to in plane_peers(q):
+            push(total.at[q, mine(q)], total.at[q, mine(q)], 2, q, to)
+
+    def gather_axis(q):
+        n = pl.ds(0, len(plane) * narrow)
+        pltpu.make_async_copy(total.at[q, n], total.at[q, n], ar_recv.at[2, q]).wait()
+        s = span(coord[q] * wide, wide)
         for d in range(1, side):
-            c, to = along(axis, d)
-            pltpu.make_async_remote_copy(
-                total.at[q, s], total.at[q, s], ar_send.at[3 + j, q], ar_recv.at[3 + j, q],
-                device_id={'ep': to}, device_id_type=MESH).start()
-
-    def gather_wait(q, j):
-        n = (side - 1) * size[j]
-        pltpu.make_async_copy(total.at[q, pl.ds(0, n)], total.at[q, pl.ds(0, n)], ar_recv.at[3 + j, q]).wait()
-
-    for q in range(3):
-        scatter(q, 0)
+            c = shifted(q, d)
+            push(total.at[q, s], total.at[q, s], 3, q, me + (c - coord[q]) * weight[q])
+
+    def gathered(q):
+        n = pl.ds(0, (side - 1) * wide)
+        pltpu.make_async_copy(total.at[q, n], total.at[q, n], ar_recv.at[3, q]).wait()
+
+    for q in range(3):
+        scatter_axis(q)
+    start_exchange(2, 1, send_f, recv_f, 1, 2)
     wait_exchange(2, 0, send_f, recv_f)
     expert_forward(0)
+    for q in range(3):
+        scatter_plane(q)
     start_exchange(4, 0, send_of, back_of, 0, 2)
     wait_exchange(2, 1, send_f, recv_f)
     expert_forward(1)
-    for j in range(3):
-        for q in range(3):
-            scatter_wait(q, j)
-            add(q, j)
-            if j < 2:
-                scatter(q, j + 1)
-            else:
-                gather(q, 2)
-        start_exchange(4, (j + 1) // 2, send_of, back_of, (j + 1) % 2, 2)
-    for j in (2, 1):
-        for q in range(3):
-            gather_wait(q, j)
-            gather(q, j - 1)
+    for q in range(3):
+        gather_plane(q)
+    start_exchange(4, 0, send_of, back_of, 1, 2)
+    start_exchange(4, 1, send_of, back_of, 0, 2)
+    for q in range(3):
+        gather_axis(q)
+    start_exchange(4, 1, send_of, back_of, 1, 2)
 
     combine_half(4, 0, send_of, back_of, slot_f, gz_f)
     wait_exchange(4, 1, send_of, back_of)
@@ -389,7 +396,7 @@
 
     late = []
     for q in range(3):
-        gather_wait(q, 0)
+        gathered(q)
         late.append(pltpu.make_async_copy(total.at[q, pl.ds(0, hid)], dwin_out.at[:, pl.ds(q * cols, cols)], out_sem.at[3 + q]))
         late[-1].start()
         turned[q * cols:(q + 1) * cols, :] = jnp.transpose(total[q, hid:, :])
@@ -399,11 +406,9 @@
     for x, src in enumerate((send_d, send_z, send_f, send_dz, send_of)):
         for j in range(2):
             drain_exchange(x, j, src)
-    for j in range(3):
-        for q in range(3):
-            n = pl.ds(0, (side - 1) * size[j])
-            pltpu.make_async_copy(total.at[q, n], total.at[q, n], ar_send.at[j, q]).wait()
-            pltpu.make_async_copy(total.at[q, n], total.at[q, n], ar_send.at[3 + j, q]).wait()
+    for q in range(3):
+        for phase, n in enumerate(((side - 1) * wide, len(plane) * narrow, len(plane) * narrow, (side - 1) * wide)):
+            pltpu.make_async_copy(total.at[q, pl.ds(0, n)], total.at[q, pl.ds(0, n)], ar_send.at[phase, q]).wait()
     for c in early + late:
         c.wait()
     send_dx.wait()
@@ -471,10 +476,10 @@
             + [route] * 2 + [rows] * 6 + [slots] * 10
             + [pltpu.VMEM(w.shape, F32) for w in (w_gate, w_up, w_down)] + [pltpu.VMEM((hid, eff), F32)]
             + [pltpu.VMEM((3, 2 * hid, cols), F32)] * 2
-            + [pltpu.VMEM((3, side - 1, 2 * hid // side ** j, cols), F32) for j in (1, 2, 3)]
+            + [pltpu.VMEM((3, side ** j - 1, 2 * hid // side ** (2 * j - 1), cols), F32) for j in (1, 2)]
             + [pltpu.VMEM((ff, hid), F32)]
             + [rows, pltpu.VMEM((tok, ff), BF16), pltpu.VMEM((tok, ff), F32), pltpu.VMEM((tok, hid), F32), pltpu.VMEM((tok, hid), F32)]
-            + [dma((5, 2)), dma((5, 2)), dma((5, 2)), dma((6, 3)), dma((6, 3)), dma((2,)), dma((2,)), dma((7,))],
+            + [dma((5, 2)), dma((5, 2)), dma((5, 2)), dma((4, 3)), dma((4, 3)), dma((2,)), dma((2,)), dma((7,))],
             compiler_params=pltpu.CompilerParams(collective_id=0, has_side_effects=True, vmem_limit_bytes=63 * MIB),
         )(ids_f, gate_f, ids_b, gate_b, *big)
         y_next, dx_prev, dw_in, dw_out, dw_gate, dw_up, dw_down = write(*results)

time: 176 us -> 185 us (1.051)
  Pallas kernels: 175 us -> 184 us
    pallas_call x1, Pallas kernels: 170 us -> 179 us  [body(): pl.pallas_call(functools.partial(step_kernel, cfg), out_shape=[jax.ShapeD...]
where the time goes in v6:
time: 185 us
  Pallas kernels  184 us (99%)
    pallas_call x1, Pallas kernels, body(): pl.pallas_call(functools.partial(step_kernel, cfg), out_shape=[jax.ShapeD...  179 us
    pallas_call x1, Pallas kernels, write(): pl.pallas_call(functools.partial(write_kernel, n), out_shape=shapes, in_s...  5.11 us

profile of v6, /device:TPU:1, one launch (start us, length us, event | category | flops | bytes accessed | tf_op | source)
XLA Modules:
  0.0 184.6 jit_solution(14717623914010598908)
XLA Ops:
  0.6 178.7 %shard_map.171 = (bf16[2048,256]{1,0:T(8,128)(2,1)}, bf16[2048,256]{1,0:T(8,128)(2,1)}, f32[256,768]{1,0:T(8,128)}, f32[768,256]{1,0:T(8,128)}, f32[2,256,384]{2...) custom-call(s32[1,2048]{1,0:T(1,128)} %bitcast.27, bf16[1,2048]{1,0:T(2,128)(2,1)} %bitcast.28, ...), custom_call_target="tpu_custom_call" | custom-call | tf_op jit(solution)/shard_map/pallas_call | solution.py:470
  179.4 5.1 %shard_map.172 = (bf16[2048,256]{1,0:T(8,128)(2,1)}, bf16[2048,256]{1,0:T(8,128)(2,1)}, f32[256,768]{1,0:T(8,128)}, f32[768,256]{1,0:T(8,128)}, f32[2,256,384]{2...) custom-call(bf16[2048,256]{1,0:T(8,128)(2,1)} %get-tuple-element.21.refs_0_, ...), custom_call_target="tpu_custom_call" | custom-call | tf_op jit(solution)/shard_map/pallas_call | solution.py:434

commit v7 on v5

--- a/solution.py
+++ b/solution.py
@@ -93,7 +93,7 @@
 
 
 def step_kernel(cfg, *refs):
-    n_pp, n_ep, side, tok, n_exp, cap, blk, chunk, eblk = cfg
+    n_pp, n_ep, side, tok, n_exp, cap, blk, chunk, eblk, pblk = cfg
     refs = list(refs)
 
     def take(n):
@@ -260,8 +260,8 @@
         wait_exchange(1, e, send_z, recv_z)
         expert_backward(e)
         start_exchange(3, e, send_dz, back_dz)
-    for e in range(2):
-        start_exchange(2, e, send_f, recv_f)
+        start_exchange(2, 0, send_f, recv_f, e, 2)
+    start_exchange(2, 1, send_f, recv_f)
     early = [pltpu.make_async_copy(a, b, out_sem.at[i]) for i, (a, b) in enumerate(((dwg, dwg_out), (dwu, dwu_out), (dwd, dwd_out)))]
     for c in early:
         c.start()
@@ -273,17 +273,17 @@
     def combine_half(x, j, src, back, slot, acc):
         wait_exchange(x, j, src, back)
 
-        @pl.loop(0, tok // blk)
+        @pl.loop(0, tok // pblk)
         def _(i):
-            t = pl.ds(pl.multiple_of(i * blk, blk), blk)
+            t = pl.ds(pl.multiple_of(i * pblk, pblk), pblk)
             acc[t, :] = combine(slot[:, t], back, j)
 
     combine_half(3, 0, send_dz, back_dz, slot_b, gz_b)
     wait_exchange(3, 1, send_dz, back_dz)
 
-    @pl.loop(0, tok // blk)
+    @pl.loop(0, tok // pblk)
     def _(i):
-        t = pl.ds(pl.multiple_of(i * blk, blk), blk)
+        t = pl.ds(pl.multiple_of(i * pblk, pblk), pblk)
         gz = gz_b[t, :] + combine(slot_b[:, t], back_dz, 1)
         h = h_b[t, :].astype(F32)
         dh = grad[t, :].astype(F32) + rms_vjp(h, inv_rms(h), gz)
@@ -378,9 +378,9 @@
     combine_half(4, 0, send_of, back_of, slot_f, gz_f)
     wait_exchange(4, 1, send_of, back_of)
 
-    @pl.loop(0, tok // blk)
+    @pl.loop(0, tok // pblk)
     def _(i):
-        t = pl.ds(pl.multiple_of(i * blk, blk), blk)
+        t = pl.ds(pl.multiple_of(i * pblk, pblk), pblk)
         picked = gz_f[t, :] + combine(slot_f[:, t], back_of, 1)
         y[t, :] = (h_f[t, :].astype(F32) + picked * column(gate_f[:, t].astype(F32))).astype(BF16)
 
@@ -452,7 +452,8 @@
         blk = min(256, tok)
         chunk = min(512, n_ep * cap)
         eblk = min(512, n_ep * cap)
-        cfg = (n_pp, n_ep, side, tok, n_exp, cap, blk, chunk, eblk)
+        pblk = min(512, tok)
+        cfg = (n_pp, n_ep, side, tok, n_exp, cap, blk, chunk, eblk, pblk)
         ids_f, ids_b = ids_fwd.reshape(1, tok), ids_bwd.reshape(1, tok)
         gate_f, gate_b = gates_fwd.reshape(1, tok), gates_bwd.reshape(1, tok)
         big = [grad_out, x_saved, w_in, w_out, x_fwd, w_gate, w_up, w_down]

time: 176 us -> 173 us (0.983)
  Pallas kernels: 175 us -> 171 us
    pallas_call x1, Pallas kernels: 170 us -> 165 us  [body(): pl.pallas_call(functools.partial(step_kernel, cfg), out_shape=[jax.ShapeD...]
where the time goes in v7:
time: 173 us; the launch traced here: 171 us
  Pallas kernels  171 us (99%)
    pallas_call x1, Pallas kernels, body(): pl.pallas_call(functools.partial(step_kernel, cfg), out_shape=[jax.ShapeD...  165 us
    pallas_call x1, Pallas kernels, write(): pl.pallas_call(functools.partial(write_kernel, n), out_shape=shapes, in_s...  5.11 us

profile of v7, /device:TPU:1, one launch (start us, length us, event | category | flops | bytes accessed | tf_op | source)
XLA Modules:
  0.0 171.3 jit_solution(2626484169139155592)
XLA Ops:
  0.6 165.4 %shard_map.171 = (bf16[2048,256]{1,0:T(8,128)(2,1)}, bf16[2048,256]{1,0:T(8,128)(2,1)}, f32[256,768]{1,0:T(8,128)}, f32[768,256]{1,0:T(8,128)}, f32[2,256,384]{2...) custom-call(s32[1,2048]{1,0:T(1,128)} %bitcast.27, bf16[1,2048]{1,0:T(2,128)(2,1)} %bitcast.28, ...), custom_call_target="tpu_custom_call" | custom-call | tf_op jit(solution)/shard_map/pallas_call | solution.py:466
  166.1 5.1 %shard_map.172 = (bf16[2048,256]{1,0:T(8,128)(2,1)}, bf16[2048,256]{1,0:T(8,128)(2,1)}, f32[256,768]{1,0:T(8,128)}, f32[768,256]{1,0:T(8,128)}, f32[2,256,384]{2...) custom-call(bf16[2048,256]{1,0:T(8,128)(2,1)} %get-tuple-element.21.refs_0_, ...), custom_call_target="tpu_custom_call" | custom-call | tf_op jit(solution)/shard_map/pallas_call | solution.py:429
